TPU v7x, 8 devices: a whole 2x2x1 slice. The times are simulated.
8 devices in a mesh: data: 8 (over z, y, x, core).
Axes of the slice: x: 2, y: 2, z: 1, core: 2. Of those that a mesh axis runs over, the one named last changes fastest.
Arguments:
- act_in: bfloat16 [32768, 768], P('data')
- grad_out: bfloat16 [32768, 768], P('data')
- w_up: bfloat16 [2, 768, 3072], replicated
- w_down: bfloat16 [2, 3072, 768], replicated
- master_up: float32 [2, 768, 3072], P(None, 'data')
- master_down: float32 [2, 3072, 768], P(None, 'data')
- exp_avg_up: float32 [2, 768, 3072], P(None, 'data')
- exp_avg_down: float32 [2, 3072, 768], P(None, 'data')
- exp_sq_up: float32 [2, 768, 3072], P(None, 'data')
- exp_sq_down: float32 [2, 3072, 768], P(None, 'data')
- learn_rate: float32 [], replicated
- clip_norm: float32 [], replicated
Outputs:
- output 1: bfloat16 [2, 768, 3072], replicated
- output 2: bfloat16 [2, 3072, 768], replicated
- output 3: float32 [2, 768, 3072], P(None, 'data')
- output 4: float32 [2, 3072, 768], P(None, 'data')
- output 5: float32 [2, 768, 3072], P(None, 'data')
- output 6: float32 [2, 3072, 768], P(None, 'data')
- output 7: float32 [2, 768, 3072], P(None, 'data')
- output 8: float32 [2, 3072, 768], P(None, 'data')
- output 9: float32 [], replicated
All inputs are finite; a program needn't handle non-finite values.
Results may differ from a plain program's by a relative error of at most 0.00406.
Values are sent between devices in bfloat16 or wider.
A program may use at most 1 GiB of HBM per device.

v0:
```python
import jax
import jax.numpy as jnp
from jax import lax
from jax.sharding import PartitionSpec as P

STEP = 10
BETA_ONE = 0.9
BETA_TWO = 0.95
ADAM_EPS = 1e-8
NORM_EPS = 1e-6
INV_SQRT_TWO = 0.7071067811865476
INV_SQRT_TWO_PI = 0.3989422804014327


def gelu_parts(pre_act):
    normal_cdf = 0.5 * (1.0 + lax.erf(pre_act * INV_SQRT_TWO))
    normal_pdf = jnp.exp(-0.5 * pre_act * pre_act) * INV_SQRT_TWO_PI
    return pre_act * normal_cdf, normal_cdf + pre_act * normal_pdf


def local_grads(act_in, grad_out, w_up, w_down):
    z_one = jnp.einsum("td,df->tf", act_in, w_up[0], preferred_element_type=jnp.float32)
    gelu_one, slope_one = gelu_parts(z_one)
    act_one = gelu_one.astype(jnp.bfloat16)
    hidden = jnp.einsum("tf,fd->td", act_one, w_down[0], preferred_element_type=jnp.float32).astype(jnp.bfloat16)
    z_three = jnp.einsum("td,df->tf", hidden, w_up[1], preferred_element_type=jnp.float32)
    gelu_three, slope_three = gelu_parts(z_three)
    act_three = gelu_three.astype(jnp.bfloat16)
    g_four = jnp.einsum("tf,td->fd", act_three, grad_out, preferred_element_type=jnp.float32)
    dz_three = (jnp.einsum("td,fd->tf", grad_out, w_down[1], preferred_element_type=jnp.float32) * slope_three).astype(jnp.bfloat16)
    g_three = jnp.einsum("td,tf->df", hidden, dz_three, preferred_element_type=jnp.float32)
    d_hidden = jnp.einsum("tf,df->td", dz_three, w_up[1], preferred_element_type=jnp.float32).astype(jnp.bfloat16)
    g_two = jnp.einsum("tf,td->fd", act_one, d_hidden, preferred_element_type=jnp.float32)
    dz_one = (jnp.einsum("td,fd->tf", d_hidden, w_down[0], preferred_element_type=jnp.float32) * slope_one).astype(jnp.bfloat16)
    g_one = jnp.einsum("td,tf->df", act_in, dz_one, preferred_element_type=jnp.float32)
    return g_one, g_two, g_three, g_four


def adam_direction(exp_avg, exp_sq, grad, clip_scale):
    bias_one = 1.0 - BETA_ONE ** STEP
    bias_two = 1.0 - BETA_TWO ** STEP
    avg_new = BETA_ONE * exp_avg + (1.0 - BETA_ONE) * clip_scale * grad
    sq_new = BETA_TWO * exp_sq + (1.0 - BETA_TWO) * (clip_scale * clip_scale) * (grad * grad)
    direction = (avg_new / bias_one) / (jnp.sqrt(sq_new / bias_two) + ADAM_EPS)
    return avg_new, sq_new, direction


def sum_squares(stacked):
    return jnp.sum(stacked * stacked, axis=(1, 2))


def solution(mesh):
    group_size = mesh.shape["data"]
    batch_rows = P("data", None)
    state_rows = P(None, "data", None)
    replicated = P()

    def reduce_rows(grad):
        return lax.psum_scatter(grad, "data", scatter_dimension=0, tiled=True) / group_size

    def device_step(act_in, grad_out, w_up, w_down, master_up, master_down, exp_avg_up, exp_avg_down, exp_sq_up, exp_sq_down, learn_rate, clip_norm):
        g_one, g_two, g_three, g_four = local_grads(act_in, grad_out, w_up, w_down)
        shard_four = reduce_rows(g_four)
        shard_three = reduce_rows(g_three)
        shard_two = reduce_rows(g_two)
        shard_one = reduce_rows(g_one)
        grad_up = jnp.stack([shard_one, shard_three])
        grad_down = jnp.stack([shard_two, shard_four])
        local_sq = jnp.sum(grad_up * grad_up) + jnp.sum(grad_down * grad_down)
        grad_norm = jnp.sqrt(lax.psum(local_sq, "data"))
        clip_scale = jnp.minimum(1.0, clip_norm / (grad_norm + NORM_EPS))
        avg_up, sq_up, dir_up = adam_direction(exp_avg_up, exp_sq_up, grad_up, clip_scale)
        avg_down, sq_down, dir_down = adam_direction(exp_avg_down, exp_sq_down, grad_down, clip_scale)
        local_stats = jnp.concatenate([sum_squares(master_up), sum_squares(master_down), sum_squares(dir_up), sum_squares(dir_down)])
        norm_stats = lax.psum(local_stats, "data")
        trust_ratio = jnp.sqrt(norm_stats[0:4]) / jnp.sqrt(norm_stats[4:8])
        master_up_out = master_up - learn_rate * trust_ratio[0:2, None, None] * dir_up
        master_down_out = master_down - learn_rate * trust_ratio[2:4, None, None] * dir_down
        new_w_up = lax.all_gather(master_up_out.astype(jnp.bfloat16), "data", axis=1, tiled=True)
        new_w_down = lax.all_gather(master_down_out.astype(jnp.bfloat16), "data", axis=1, tiled=True)
        return (new_w_up, new_w_down, master_up_out, master_down_out, avg_up, avg_down, sq_up, sq_down, grad_norm)

    return jax.shard_map(device_step, mesh=mesh, in_specs=(batch_rows, batch_rows, replicated, replicated, state_rows, state_rows, state_rows, state_rows, state_rows, state_rows, replicated, replicated), out_specs=(replicated, replicated, state_rows, state_rows, state_rows, state_rows, state_rows, state_rows, replicated), check_vma=False)
```

profile of v0, /device:TPU:0, one launch (start us, length us, event | category | flops | bytes accessed | tf_op | source)
XLA Modules:
  0.0 690.0 jit_solution(3621240949085241777)
XLA Ops:
  7.3 38.5 %multiply_convert_fusion.1 = (bf16[4096,3072]{1,0:T(8,128)(2,1)}, f32[4096,3072]{1,0:T(8,128)}) fusion(bf16[4096,768]{1,0:T(8,128)(2,1)} %param.12, bf16[2,768,3072]{2,1,0:T(8,128)(2,1)} %param.14), kind=kOutput, calls=%fused_computation.16 | convolution fusion | flops 19390267392 | bytes 86507520 | tf_op jit(solution)/shard_map/td,df->tf/dot_general | solution.py:22
  45.7 24.4 %convolution_convert_fusion.1 = bf16[4096,768]{1,0:T(8,128)(2,1)} fusion(bf16[4096,3072]{1,0:T(8,128)(2,1)} %get-tuple-element.39, bf16[2,3072,768]{2,1,0:T(8,128)(2,1)S(1)} %copy-done.11), kind=kOutput, calls=%fused_computation.20 | convolution fusion | flops 19330498560 | bytes 36175872 | tf_op jit(solution)/shard_map/tf,fd->td/dot_general | solution.py:25
  70.2 26.9 %fusion.14 = f32[4096,3072]{1,0:T(8,128)} fusion(bf16[4096,768]{1,0:T(8,128)(2,1)} %convolution_convert_fusion.1, bf16[2,768,3072]{2,1,0:T(8,128)(2,1)S(1)} %bitcast.71), kind=kOutput, calls=%fused_computation.23 | convolution fusion | flops 19327352832 | bytes 61341696 | tf_op jit(solution)/shard_map/td,df->tf/dot_general | solution.py:26
  97.1 42.9 %fusion.5 = bf16[4096,3072]{1,0:T(8,128)(2,1)} fusion(f32[4096,3072]{1,0:T(8,128)} %fusion.14, bf16[4096,768]{1,0:T(8,128)(2,1)} %param.13, bf16[2,3072,768]{2,1,0:T(8,128)(2,1)} %param.15), kind=kOutput, calls=%fused_computation.7 | convolution fusion | flops 19453181952 | bytes 86507520 | tf_op jit(solution)/shard_map/td,fd->tf/dot_general | solution.py:30
  140.0 25.2 %fusion.29 = f32[768,3072]{1,0:T(8,128)} fusion(bf16[4096,768]{1,0:T(8,128)(2,1)S(1)} %copy-done.12, bf16[4096,3072]{1,0:T(8,128)(2,1)} %fusion.5), kind=kOutput, calls=%fused_computation.62 | convolution fusion | flops 19327352832 | bytes 40894464
  165.3 26.2 %convolution_convert_fusion = bf16[4096,768]{1,0:T(8,128)(2,1)} fusion(bf16[4096,3072]{1,0:T(8,128)(2,1)} %fusion.5, bf16[2,768,3072]{2,1,0:T(8,128)(2,1)} %param.14), kind=kOutput, calls=%fused_computation.19 | convolution fusion | flops 19330498560 | bytes 36175872 | tf_op jit(solution)/shard_map/tf,df->td/dot_general | solution.py:32
  191.5 42.8 %fusion.66 = bf16[4096,3072]{1,0:T(8,128)(2,1)} fusion(f32[4096,3072]{1,0:T(8,128)} %get-tuple-element.40, bf16[2,3072,768]{2,1,0:T(8,128)(2,1)} %param.15, bf16[4096,768]{1,0:T(8,128)(2,1)} %convolution_convert_fusion), kind=kOutput, calls=%bitcast_fusion.5.clone.1 | convolution fusion | flops 19453181952 | bytes 86507520 | tf_op jit(solution)/shard_map/td,fd->tf/dot_general | solution.py:34
  234.3 25.2 %convolution_bitcast_fusion = f32[768,3072]{0,1:T(8,128)} fusion(bf16[4096,768]{1,0:T(8,128)(2,1)S(1)} %bitcast.73, bf16[4096,3072]{1,0:T(8,128)(2,1)} %fusion.66), kind=kOutput, calls=%fused_computation.21 | convolution fusion | flops 19327352832 | bytes 40894464 | tf_op jit(solution)/shard_map/td,tf->df/dot_general | solution.py:35
  259.5 9.6 %copy.39 = f32[768,3072]{1,0:T(8,128)} copy(f32[768,3072]{0,1:T(8,128)} %convolution_bitcast_fusion) | data formatting | bytes 18874368
  269.1 26.6 %fusion.30 = f32[3072,768]{1,0:T(8,128)} fusion(bf16[4096,3072]{1,0:T(8,128)(2,1)} %get-tuple-element.39, bf16[4096,768]{1,0:T(8,128)(2,1)} %convolution_convert_fusion), kind=kOutput, calls=%fused_computation.63 | convolution fusion | flops 19327352832 | bytes 40894464 | tf_op jit(solution)/shard_map/tf,td->fd/dot_general | solution.py:33
  295.8 29.0 %fusion.12 = f32[3072,768]{1,0:T(8,128)} fusion(bf16[4096,768]{1,0:T(8,128)(2,1)} %param.13, f32[4096,3072]{1,0:T(8,128)} %fusion.14), kind=kOutput, calls=%fused_computation.18 | convolution fusion | flops 19390267392 | bytes 66060288 | tf_op jit(solution)/shard_map/tf,td->fd/dot_general | solution.py:29
  331.3 8.2 %reduce-scatter.13.cloned.1.call-done = f32[96,3072]{1,0:T(8,128)} async-done(((f32[768,3072]{1,0:T(8,128)}), f32[96,3072]{1,0:T(8,128)}) %reduce-scatter.13.cloned.1.call-update) | async-done | bytes 1179664
  345.0 65.4 %reduce-scatter.9.cloned.1.call-done = f32[384,768]{1,0:T(8,128)} async-done(((f32[3072,768]{1,0:T(8,128)}), f32[384,768]{1,0:T(8,128)}) %reduce-scatter.9.cloned.1.call-update) | async-done | bytes 1179664 | tf_op jit(solution)/shard_map/reduce_scatter | solution.py:59
  411.8 69.9 %reduce-scatter.11.cloned.1.call-done = f32[384,768]{1,0:T(8,128)} async-done(((f32[3072,768]{1,0:T(8,128)}), f32[384,768]{1,0:T(8,128)}) %reduce-scatter.11.cloned.1.call-update) | async-done | bytes 1179664 | tf_op jit(solution)/shard_map/reduce_scatter | solution.py:59
  488.9 22.2 %psum.14 = f32[]{:T(128)} all-reduce(f32[]{:T(128)S(6)} %add.58), channel_id=1, replica_groups=mesh['data'=8] {'data'}, use_global_device_ids=true, to_apply=%region_8.0 | all-reduce | flops 1 | bytes 8 | tf_op jit(solution)/shard_map/psum | solution.py:70
  511.9 7.0 %multiply_reduce_fusion = (f32[2]{0:T(128)S(1)}, f32[2,96,3072]{1,2,0:T(8,128)}, f32[2,96,3072]{1,2,0:T(8,128)S(1)}) fusion(f32[1,96,3072]{1,2,0:T(8,128)} %copy-done, f32[1,96,3072]{1,2,0:T(8,128)} %copy-done.1, f32[]{:T(128)S(6)} %mul.179, f32[2,96,3072]{1,2,0:T(8,128)} %copy.29, f32[]{:T(128)S(6)} %mul.185, f32[2,96,3072]{1,2,0:T(8,128)} %copy.31), kind=kLoop, calls=%fused_computation.38 | loop fusion | flops 8257534 | bytes 11796496 | tf_op jit(solution)/shard_map/reduce_sum | solution.py:49
  524.1 24.4 %psum.15 = f32[8]{0:T(128)S(1)} all-reduce(f32[8]{0:T(128)S(1)} %pad_maximum_fusion.2), channel_id=1, replica_groups=mesh['data'=8] {'data'}, use_global_device_ids=true, to_apply=%region_11.0 | all-reduce | flops 8 | bytes 64 | tf_op jit(solution)/shard_map/psum | solution.py:75
  548.7 6.0 fusion.27
  558.2 6.6 fusion.28
  564.7 3.9 copy.33
  577.6 31.0 %all-gather.5.cloned.1.call-done = bf16[2,3072,768]{2,1,0:T(8,128)(2,1)} async-done(((bf16[2,384,768]{2,1,0:T(8,128)(2,1)}), bf16[2,3072,768]{2,1,0:T(8,128)(2,1)}) %all-gather.5.cloned.1.call-update) | async-done | bytes 9437200 | tf_op jit(solution)/shard_map/all_gather | solution.py:80
  608.6 54.6 %all-gather.3.cloned.1.call-done = bf16[2,768,3072]{2,0,1:T(2,128)(2,1)} async-done(((bf16[2,96,3072]{2,0,1:T(2,128)(2,1)}), bf16[2,768,3072]{2,0,1:T(2,128)(2,1)}) %all-gather.3.cloned.1.call-update) | async-done | bytes 9437200 | tf_op jit(solution)/shard_map/all_gather | solution.py:79
  663.3 10.3 %copy.34 = bf16[2,768,3072]{2,1,0:T(8,128)(2,1)} copy(bf16[2,768,3072]{2,0,1:T(2,128)(2,1)} %all-gather.3.cloned.1.call-done) | data formatting | bytes 18874368
  673.6 8.0 %copy.46 = bf16[2,3072,768]{2,1,0:T(8,128)(2,1)} copy(bf16[2,3072,768]{2,1,0:T(8,128)(2,1)} %all-gather.5.cloned.1.call-done) | data formatting | bytes 18874368
  (70 shorter events, 35.7 us)
Async XLA Ops:
  7.2 322.3 %reduce-scatter.15.cloned.1.call-start = ((), (), s32[]{:S(2)}) async-start(), calls=%async_computation.9 | async-start | bytes 10616832
  7.2 38.5 %copy-start.11 = (bf16[2,3072,768]{2,1,0:T(8,128)(2,1)S(1)}, bf16[2,3072,768]{2,1,0:T(8,128)(2,1)}, u32[]{:S(2)}) copy-start(bf16[2,3072,768]{2,1,0:T(8,128)(2,1)} %param.15) | copy-start | bytes 28311556
  7.2 62.9 %slice-start = ((s8[9437184]{0:T(1024)(128)(4,1)}), s8[4194304]{0:T(1024)(128)(4,1)S(1)}, s32[]{:S(2)}) async-start(s8[9437184]{0:T(1024)(128)(4,1)} %bitcast.70), calls=%async_computation.10 | async-start | bytes 8388608
  7.2 62.9 %slice-start.1 = ((s8[9437184]{0:T(1024)(128)(4,1)}), s8[4194304]{0:T(1024)(128)(4,1)S(1)}, s32[]{:S(2)}) async-start(s8[9437184]{0:T(1024)(128)(4,1)} %bitcast.70), calls=%async_computation.11 | async-start | bytes 8388608
  45.7 24.4 %slice-start.2 = ((s8[9437184]{0:T(1024)(128)(4,1)}), s8[1048576]{0:T(1024)(128)(4,1)S(1)}, s32[]{:S(2)}) async-start(s8[9437184]{0:T(1024)(128)(4,1)} %bitcast.70), calls=%async_computation.12 | async-start | bytes 2097152
  97.1 42.9 %copy-start.12 = (bf16[4096,768]{1,0:T(8,128)(2,1)S(1)}, bf16[4096,768]{1,0:T(8,128)(2,1)}, u32[]{:S(2)}) copy-start(bf16[4096,768]{1,0:T(8,128)(2,1)} %convolution_convert_fusion.1) | copy-start | bytes 18874372
  165.2 174.3 %reduce-scatter.13.cloned.1.call-start = ((), (), s32[]{:S(2)}) async-start(), calls=%async_computation.8 | async-start | bytes 10616832
  165.3 69.0 %slice-start.3 = ((s8[6291456]{0:T(1024)(128)(4,1)}), s8[4194304]{0:T(1024)(128)(4,1)S(1)}, s32[]{:S(2)}) async-start(s8[6291456]{0:T(1024)(128)(4,1)} %bitcast.72), calls=%async_computation.13 | async-start | bytes 8388608
  191.5 42.8 %slice-start.4 = ((s8[6291456]{0:T(1024)(128)(4,1)}), s8[2097152]{0:T(1024)(128)(4,1)S(1)}, s32[]{:S(2)}) async-start(s8[6291456]{0:T(1024)(128)(4,1)} %bitcast.72), calls=%async_computation.14 | async-start | bytes 4194304
  269.1 141.3 %reduce-scatter.9.cloned.1.call-start = ((), (), s32[]{:S(2)}) async-start(), calls=%async_computation.4 | async-start | bytes 10616832 | tf_op jit(solution)/shard_map/reduce_scatter | solution.py:59
  295.8 186.0 %reduce-scatter.11.cloned.1.call-start = ((), (), s32[]{:S(2)}) async-start(), calls=%async_computation.5 | async-start | bytes 10616832 | tf_op jit(solution)/shard_map/reduce_scatter | solution.py:59
  324.9 4.2 copy-start.6
  324.9 283.8 %all-gather.5.cloned.1.call-start = ((), (), s32[]{:S(2)}) async-start(), calls=%async_computation.7 | async-start | bytes 10616832 | tf_op jit(solution)/shard_map/all_gather | solution.py:80
  341.3 1.1 copy-start
  342.5 1.1 copy-start.1
  343.6 143.0 %copy-start.8 = (f32[2,96,3072]{2,1,0:T(8,128)S(1)}, f32[2,96,3072]{2,1,0:T(8,128)}, u32[]{:S(2)}) copy-start(f32[2,96,3072]{2,1,0:T(8,128)} %param.20) | copy-start | bytes 7077892
  411.8 77.2 %copy-start.2 = (f32[1,384,768]{2,1,0:T(8,128)}, f32[1,384,768]{2,1,0:T(8,128)S(1)}, u32[]{:S(2)}) copy-start(f32[1,384,768]{2,1,0:T(8,128)S(1)} %multiply_bitcast_fusion.3) | copy-start | bytes 3538948
  483.1 1.0 copy-start.4
  511.9 7.0 %copy-start.3 = (f32[1,384,768]{2,1,0:T(8,128)S(1)}, f32[1,384,768]{2,1,0:T(8,128)}, u32[]{:S(2)}) copy-start(f32[1,384,768]{2,1,0:T(8,128)} %copy-done.2) | copy-start | bytes 3538948
  511.9 7.0 %copy-start.5 = (f32[1,384,768]{2,1,0:T(8,128)S(1)}, f32[1,384,768]{2,1,0:T(8,128)}, u32[]{:S(2)}) copy-start(f32[1,384,768]{2,1,0:T(8,128)} %copy-done.4) | copy-start | bytes 3538948
  511.9 7.0 %copy-start.7 = (f32[2,384,768]{2,1,0:T(8,128)S(1)}, f32[2,384,768]{2,1,0:T(8,128)}, u32[]{:S(2)}) copy-start(f32[2,384,768]{2,1,0:T(8,128)} %param.17) | copy-start | bytes 7077892
  511.9 7.0 %copy-start.9 = (f32[2,384,768]{2,1,0:T(8,128)S(1)}, f32[2,384,768]{2,1,0:T(8,128)}, u32[]{:S(2)}) copy-start(f32[2,384,768]{2,1,0:T(8,128)} %param.19) | copy-start | bytes 7077892
  511.9 7.6 %copy-start.10 = (f32[2,384,768]{2,1,0:T(8,128)S(1)}, f32[2,384,768]{2,1,0:T(8,128)}, u32[]{:S(2)}) copy-start(f32[2,384,768]{2,1,0:T(8,128)} %param.21) | copy-start | bytes 7077892
  554.7 108.6 %all-gather.3.cloned.1.call-start = ((), (), s32[]{:S(2)}) async-start(), calls=%async_computation.6 | async-start | bytes 10616832 | tf_op jit(solution)/shard_map/all_gather | solution.py:79
Sparse Core Ops, SparseCore 0:
  165.3 70.2 reduce-scatter.14
  269.2 70.2 reduce-scatter.12
  342.9 67.4 reduce-scatter.8
  414.3 67.4 reduce-scatter.10
  554.8 53.7 all-gather.4
  610.3 52.9 all-gather.2
where the time goes:
time: 699 us; the launch traced here: 690 us
  matrix products  308 us (44%)
  waiting for transfers between devices  229 us (33%)
  local copies, waits for them, and re-layouts  57.1 us (8%)
  blocking collectives  46.6 us (7%)
  other arithmetic  29.6 us (4%)
  between operations  19.4 us (3%)
    reduce_scatter x2, waiting for transfers between devices, reduce_rows(): lax.psum_scatter(grad, 'data', scatter_dimension=0, tiled=True) / group_size  135 us
    all_gather x1, waiting for transfers between devices, device_step(): lax.all_gather(master_up_out.astype(jnp.bfloat16), 'data', axis=1, tiled=...  54.6 us
    unnamed x47, local copies, waits for them, and re-layouts  53.2 us
    dot_general x1, matrix products, local_grads(): jnp.einsum('td,fd->tf', grad_out, w_down[1], preferred_element_type=jnp.f...  42.9 us
    dot_general x1, matrix products, local_grads(): jnp.einsum('td,fd->tf', d_hidden, w_down[0], preferred_element_type=jnp.f...  42.8 us
    dot_general x1, matrix products, local_grads(): jnp.einsum('td,df->tf', act_in, w_up[0], preferred_element_type=jnp.float32)  38.5 us
    all_gather x1, waiting for transfers between devices, device_step(): lax.all_gather(master_down_out.astype(jnp.bfloat16), 'data', axis=1, tile...  31 us
    dot_general x1, matrix products, local_grads(): jnp.einsum('tf,td->fd', act_three, grad_out, preferred_element_type=jnp.f...  29 us
  transfers between devices with their start and end apart: 6, of which 5 were waited for; matrix products, arithmetic and copies ran while one was open for 28% of the time, Pallas kernels for 0%

commit v1 on v0

--- a/solution.py
+++ b/solution.py
@@ -1,6 +1,10 @@
+import functools
+
 import jax
 import jax.numpy as jnp
 from jax import lax
+from jax.experimental import pallas as pl
+from jax.experimental.pallas import tpu as pltpu
 from jax.sharding import PartitionSpec as P
 
 STEP = 10
@@ -36,13 +40,212 @@
     return g_one, g_two, g_three, g_four
 
 
-def adam_direction(exp_avg, exp_sq, grad, clip_scale):
+MESH = pl.DeviceIdType.MESH
+VMEM_LIMIT = 66 * 1024 * 1024 - 2 * 1024 * 1024
+
+
+def coords():
+    me = lax.axis_index("data")
+    core, col, row = me % 2, (me // 2) % 2, me // 4
+    return me, me + 1 - 2 * core, me + 2 - 4 * col, me + 4 - 8 * row
+
+
+def remote(src, dst, send_sem, recv_sem, device):
+    return pltpu.make_async_remote_copy(src_ref=src, dst_ref=dst, send_sem=send_sem, recv_sem=recv_sem, device_id=(device,), device_id_type=MESH)
+
+
+def meet_all(me, group_size):
+    barrier = pltpu.get_barrier_semaphore()
+    for step in range(1, group_size):
+        pl.semaphore_signal(barrier, inc=1, device_id=((me + step) % group_size,), device_id_type=MESH)
+    pl.semaphore_wait(barrier, group_size - 1)
+
+
+def exchange_start(me, group_size, slots, send_sem, recv_sem):
+    copies = []
+    for step in range(1, group_size):
+        copies.append(remote(slots.at[me], slots.at[me], send_sem.at[step], recv_sem.at[step], (me + step) % group_size))
+        copies[-1].start()
+    return copies
+
+
+def stat_sum_kernel(group_size, tile_ref, out_ref, slots, send_sem, recv_sem):
+    me = lax.axis_index("data")
+    slots[me] = tile_ref[...]
+    meet_all(me, group_size)
+    for copy in exchange_start(me, group_size, slots, send_sem, recv_sem):
+        copy.wait()
+    total = slots[0]
+    for index in range(1, group_size):
+        total = total + slots[index]
+    out_ref[...] = total
+
+
+def stat_sum(tile, group_size):
+    return pl.pallas_call(
+        functools.partial(stat_sum_kernel, group_size),
+        out_shape=jax.ShapeDtypeStruct((8, 128), jnp.float32),
+        in_specs=[pl.BlockSpec(memory_space=pltpu.VMEM)],
+        out_specs=pl.BlockSpec(memory_space=pltpu.VMEM),
+        scratch_shapes=[pltpu.VMEM((group_size, 8, 128), jnp.float32), pltpu.SemaphoreType.DMA((group_size,)), pltpu.SemaphoreType.DMA((group_size,))],
+        compiler_params=pltpu.CompilerParams(collective_id=0, has_side_effects=True),
+        name="stat_sum",
+    )(tile)
+
+
+def moments_kernel(clip_ref, g_up, g_down, m_up, m_down, v_up, v_down, m_up_out, m_down_out, v_up_out, v_down_out, u_up, u_down, stats):
     bias_one = 1.0 - BETA_ONE ** STEP
     bias_two = 1.0 - BETA_TWO ** STEP
-    avg_new = BETA_ONE * exp_avg + (1.0 - BETA_ONE) * clip_scale * grad
-    sq_new = BETA_TWO * exp_sq + (1.0 - BETA_TWO) * (clip_scale * clip_scale) * (grad * grad)
-    direction = (avg_new / bias_one) / (jnp.sqrt(sq_new / bias_two) + ADAM_EPS)
-    return avg_new, sq_new, direction
+    scale = clip_ref[0]
+    row_id = lax.broadcasted_iota(jnp.int32, (8, 128), 0)
+    sums = jnp.zeros((8, 128), jnp.float32)
+    for family, (g, m, v, m_out, v_out, u) in enumerate([(g_up, m_up, v_up, m_up_out, v_up_out, u_up), (g_down, m_down, v_down, m_down_out, v_down_out, u_down)]):
+        for layer in range(2):
+            grad = g[layer]
+            avg_new = BETA_ONE * m[layer] + (1.0 - BETA_ONE) * scale * grad
+            sq_new = BETA_TWO * v[layer] + (1.0 - BETA_TWO) * (scale * scale) * (grad * grad)
+            direction = (avg_new / bias_one) / (jnp.sqrt(sq_new / bias_two) + ADAM_EPS)
+            m_out[layer] = avg_new
+            v_out[layer] = sq_new
+            u[layer] = direction
+            sums = sums + jnp.where(row_id == 4 + 2 * family + layer, jnp.sum(direction * direction), 0.0)
+
+    @pl.when(pl.program_id(0) == 0)
+    def _():
+        stats[...] = jnp.zeros_like(stats)
+
+    stats[...] += sums
+
+
+def moments(clip_scale, g_up, g_down, m_up, m_down, v_up, v_down, steps=4):
+    up, down = g_up.shape, g_down.shape
+    up_spec = pl.BlockSpec((2, up[1] // steps, up[2]), lambda i: (0, i, 0))
+    down_spec = pl.BlockSpec((2, down[1] // steps, down[2]), lambda i: (0, i, 0))
+    pair = [up_spec, down_spec]
+    up_shape, down_shape = jax.ShapeDtypeStruct(up, jnp.float32), jax.ShapeDtypeStruct(down, jnp.float32)
+    return pl.pallas_call(
+        moments_kernel,
+        grid=(steps,),
+        out_shape=[up_shape, down_shape] * 3 + [jax.ShapeDtypeStruct((8, 128), jnp.float32)],
+        in_specs=[pl.BlockSpec(memory_space=pltpu.SMEM)] + pair * 3,
+        out_specs=pair * 3 + [pl.BlockSpec((8, 128), lambda i: (0, 0))],
+        compiler_params=pltpu.CompilerParams(dimension_semantics=("arbitrary",), vmem_limit_bytes=40 * 1024 * 1024),
+        name="moments",
+    )(clip_scale.reshape(1), g_up, g_down, m_up, m_down, v_up, v_down)
+
+
+PIECES = ((0, 0), (0, 1), (1, 0), (1, 1))
+
+
+def update_kernel(group_size, rate_ref, stats_ref, u_up, u_down, p_up, p_down, all_up, all_down, p_up_out, p_down_out,
+                  slots, w_up, w_down, stat_send, stat_recv, send_sem, recv_sem, local_sem):
+    me, partner, near_x, near_y = coords()
+    slots[me] = stats_ref[...]
+    meet_all(me, group_size)
+    for copy in exchange_start(me, group_size, slots, stat_send, stat_recv):
+        copy.wait()
+    total = slots[0]
+    for index in range(1, group_size):
+        total = total + slots[index]
+    ratio = jnp.sqrt(total[0:4]) / jnp.sqrt(total[4:8])
+    rate = rate_ref[0]
+    params = ((u_up, p_up, p_up_out, w_up, all_up), (u_down, p_down, p_down_out, w_down, all_down))
+
+    def place(piece, owner):
+        family, layer = PIECES[piece]
+        full = params[family][4]
+        rows = params[family][3].shape[1]
+        return full.at[layer, pl.ds(pl.multiple_of(owner * rows, rows), rows), :]
+
+    sends = []
+    count = [0]
+
+    def forward(src, piece, owner, device, rel):
+        copy = remote(src, place(piece, owner), send_sem.at[count[0]], recv_sem.at[rel, piece], device)
+        count[0] += 1
+        copy.start()
+        sends.append(copy)
+
+    def arrival(piece, rel, owner):
+        spot = place(piece, owner)
+        remote(spot, spot, send_sem.at[0], recv_sem.at[rel, piece], me).wait_recv()
+        return spot
+
+    own = {}
+    local = []
+    for piece in (0, 2, 1, 3):
+        family, layer = PIECES[piece]
+        u, p, p_out, w, full = params[family]
+        index = 2 * family + layer
+        new = p[layer] - rate * ratio[index:index + 1, 0:1] * u[layer]
+        p_out[layer] = new
+        w[layer] = new.astype(jnp.bfloat16)
+        own[piece] = w.at[layer]
+        if family == 0:
+            forward(own[piece], piece, me, near_x, 2)
+        else:
+            forward(own[piece], piece, me, near_y, 4)
+        forward(own[piece], piece, me, partner, 1)
+        copy = pltpu.make_async_copy(own[piece], place(piece, me), local_sem.at[piece])
+        copy.start()
+        local.append(copy)
+    for piece in (2, 3):
+        forward(own[piece], piece, me, near_x, 2)
+    for piece in (0, 1):
+        forward(own[piece], piece, me, near_y, 4)
+    diag = near_x + near_y - me
+    for k in range(2):
+        spot = arrival(k, 2, near_x)
+        forward(spot, k, near_x, near_y, 6)
+        forward(spot, k, near_x, partner, 3)
+        spot = arrival(2 + k, 4, near_y)
+        forward(spot, 2 + k, near_y, near_x, 6)
+        forward(spot, 2 + k, near_y, partner, 5)
+    for k in range(2):
+        spot = arrival(2 + k, 2, near_x)
+        forward(spot, 2 + k, near_x, partner, 3)
+        spot = arrival(k, 4, near_y)
+        forward(spot, k, near_y, partner, 5)
+    for k in range(2):
+        for piece in (2 + k, k):
+            spot = arrival(piece, 6, diag)
+            forward(spot, piece, diag, partner, 7)
+    for rel, owner in ((1, partner), (3, near_x + partner - me), (5, near_y + partner - me), (7, diag + partner - me)):
+        for piece in range(4):
+            arrival(piece, rel, owner)
+    for copy in sends:
+        copy.wait_send()
+    for copy in local:
+        copy.wait()
+
+
+def update_and_gather(group_size, learn_rate, stats, u_up, u_down, p_up, p_down):
+    up, down = p_up.shape, p_down.shape
+    vmem = pl.BlockSpec(memory_space=pltpu.VMEM)
+    hbm = pl.BlockSpec(memory_space=pl.ANY)
+    return pl.pallas_call(
+        functools.partial(update_kernel, group_size),
+        out_shape=[
+            jax.ShapeDtypeStruct((up[0], up[1] * group_size, up[2]), jnp.bfloat16),
+            jax.ShapeDtypeStruct((down[0], down[1] * group_size, down[2]), jnp.bfloat16),
+            jax.ShapeDtypeStruct(up, jnp.float32),
+            jax.ShapeDtypeStruct(down, jnp.float32),
+        ],
+        in_specs=[pl.BlockSpec(memory_space=pltpu.SMEM)] + [vmem] * 5,
+        out_specs=[hbm, hbm, vmem, vmem],
+        scratch_shapes=[
+            pltpu.VMEM((group_size, 8, 128), jnp.float32),
+            pltpu.VMEM(up, jnp.bfloat16),
+            pltpu.VMEM(down, jnp.bfloat16),
+            pltpu.SemaphoreType.DMA((group_size,)),
+            pltpu.SemaphoreType.DMA((group_size,)),
+            pltpu.SemaphoreType.DMA((32,)),
+            pltpu.SemaphoreType.DMA((group_size, 4)),
+            pltpu.SemaphoreType.DMA((4,)),
+        ],
+        compiler_params=pltpu.CompilerParams(collective_id=1, has_side_effects=True, vmem_limit_bytes=40 * 1024 * 1024),
+        name="update_and_gather",
+    )(learn_rate.reshape(1), stats, u_up, u_down, p_up, p_down)
 
 
 def sum_squares(stacked):
@@ -67,17 +270,12 @@
         grad_up = jnp.stack([shard_one, shard_three])
         grad_down = jnp.stack([shard_two, shard_four])
         local_sq = jnp.sum(grad_up * grad_up) + jnp.sum(grad_down * grad_down)
-        grad_norm = jnp.sqrt(lax.psum(local_sq, "data"))
+        grad_norm = jnp.sqrt(stat_sum(jnp.full((8, 128), local_sq), group_size)[0, 0])
         clip_scale = jnp.minimum(1.0, clip_norm / (grad_norm + NORM_EPS))
-        avg_up, sq_up, dir_up = adam_direction(exp_avg_up, exp_sq_up, grad_up, clip_scale)
-        avg_down, sq_down, dir_down = adam_direction(exp_avg_down, exp_sq_down, grad_down, clip_scale)
-        local_stats = jnp.concatenate([sum_squares(master_up), sum_squares(master_down), sum_squares(dir_up), sum_squares(dir_down)])
-        norm_stats = lax.psum(local_stats, "data")
-        trust_ratio = jnp.sqrt(norm_stats[0:4]) / jnp.sqrt(norm_stats[4:8])
-        master_up_out = master_up - learn_rate * trust_ratio[0:2, None, None] * dir_up
-        master_down_out = master_down - learn_rate * trust_ratio[2:4, None, None] * dir_down
-        new_w_up = lax.all_gather(master_up_out.astype(jnp.bfloat16), "data", axis=1, tiled=True)
-        new_w_down = lax.all_gather(master_down_out.astype(jnp.bfloat16), "data", axis=1, tiled=True)
+        master_sq = jnp.concatenate([sum_squares(master_up), sum_squares(master_down)])
+        avg_up, avg_down, sq_up, sq_down, dir_up, dir_down, dir_stats = moments(clip_scale, grad_up, grad_down, exp_avg_up, exp_avg_down, exp_sq_up, exp_sq_down)
+        stats = dir_stats + jnp.pad(master_sq, (0, 4))[:, None]
+        new_w_up, new_w_down, master_up_out, master_down_out = update_and_gather(group_size, learn_rate, stats, dir_up, dir_down, master_up, master_down)
         return (new_w_up, new_w_down, master_up_out, master_down_out, avg_up, avg_down, sq_up, sq_down, grad_norm)
 
     return jax.shard_map(device_step, mesh=mesh, in_specs=(batch_rows, batch_rows, replicated, replicated, state_rows, state_rows, state_rows, state_rows, state_rows, state_rows, replicated, replicated), out_specs=(replicated, replicated, state_rows, state_rows, state_rows, state_rows, state_rows, state_rows, replicated), check_vma=False)

time: 699 us -> 629 us (0.90)
  Pallas kernels: 0 us -> 102 us
  waiting for transfers between devices: 229 us -> 145 us
  blocking collectives: 46.6 us -> 0 us
  local copies, waits for them, and re-layouts: 57.1 us -> 32.8 us
  other arithmetic: 29.6 us -> 13.1 us
    pallas_call x0 -> x3, Pallas kernels: none -> 102 us  [the longest x1 86.4 us: update_and_gather(): pl.pallas_call(functools.partial(update_kernel, group_size), out_shape=[j...]
    all_gather x2 -> x0, waiting for transfers between devices: 85.7 us -> none  [the longest x1 54.6 us: device_step(): lax.all_gather(master_up_out.astype(jnp.bfloat16), 'data', axis=1, tiled=...]
    psum x2 -> x0, blocking collectives: 46.6 us -> none  [the longest x1 24.4 us: device_step(): norm_stats = lax.psum(local_stats, 'data')]
    unnamed x1 -> x0, matrix products: 25.2 us -> none
    dot_general x0 -> x1, matrix products: none -> 25.1 us  [local_grads(): jnp.einsum('td,tf->df', hidden, dz_three, preferred_element_type=jnp.floa...]
    unnamed x47 -> x36, local copies, waits for them, and re-layouts: 53.2 us -> 31 us
    convert_element_type x2 -> x0, other arithmetic: 12.6 us -> none  [the longest x1 6.56 us: device_step(): master_up_out.astype(jnp.bfloat16)]
    reduce_scatter x2 -> x4, waiting for transfers between devices: 135 us -> 145 us  [reduce_rows(): lax.psum_scatter(grad, 'data', scatter_dimension=0, tiled=True) / group_size]
  transfers between devices with their start and end apart: 6 -> 4, of which waited for: 5 -> 3; matrix products, arithmetic and copies ran while one was open for 28% -> 26% of each run, Pallas kernels for 0% -> 0%
where the time goes in v1:
time: 629 us; the launch traced here: 621 us
  matrix products  308 us (49%)
  waiting for transfers between devices  145 us (23%)
  Pallas kernels  102 us (16%)
  local copies, waits for them, and re-layouts  32.8 us (5%)
  between operations  19 us (3%)
  other arithmetic  13.1 us (2%)
    reduce_scatter x4, waiting for transfers between devices, reduce_rows(): lax.psum_scatter(grad, 'data', scatter_dimension=0, tiled=True) / group_size  145 us
    pallas_call x1, Pallas kernels, update_and_gather(): pl.pallas_call(functools.partial(update_kernel, group_size), out_shape=[j...  86.4 us
    dot_general x1, matrix products, local_grads(): jnp.einsum('td,fd->tf', grad_out, w_down[1], preferred_element_type=jnp.f...  43.2 us
    dot_general x1, matrix products, local_grads(): jnp.einsum('td,fd->tf', d_hidden, w_down[0], preferred_element_type=jnp.f...  42.7 us
    dot_general x1, matrix products, local_grads(): jnp.einsum('td,df->tf', act_in, w_up[0], preferred_element_type=jnp.float32)  38.6 us
    unnamed x36, local copies, waits for them, and re-layouts  31 us
    dot_general x1, matrix products, local_grads(): jnp.einsum('tf,td->fd', act_three, grad_out, preferred_element_type=jnp.f...  29.1 us
    dot_general x1, matrix products, local_grads(): jnp.einsum('td,df->tf', hidden, w_up[1], preferred_element_type=jnp.float32)  26.9 us
  transfers between devices with their start and end apart: 4, of which 3 were waited for; matrix products, arithmetic and copies ran while one was open for 26% of the time, Pallas kernels for 0%

profile of v1, /device:TPU:0, one launch (start us, length us, event | category | flops | bytes accessed | tf_op | source)
XLA Modules:
  0.0 621.0 jit_solution(13511236419247393406)
XLA Ops:
  7.3 38.6 %multiply_convert_fusion.1 = (bf16[4096,3072]{1,0:T(8,128)(2,1)}, f32[4096,3072]{1,0:T(8,128)}) fusion(bf16[4096,768]{1,0:T(8,128)(2,1)} %param.12, bf16[2,768,3072]{2,1,0:T(8,128)(2,1)} %param.14), kind=kOutput, calls=%fused_computation.16 | convolution fusion | flops 19390267392 | bytes 86507520 | tf_op jit(solution)/shard_map/td,df->tf/dot_general | solution.py:26
  45.8 24.4 %convolution_convert_fusion.1 = bf16[4096,768]{1,0:T(8,128)(2,1)} fusion(bf16[4096,3072]{1,0:T(8,128)(2,1)} %get-tuple-element.35, bf16[2,3072,768]{2,1,0:T(8,128)(2,1)S(1)} %copy-done.9), kind=kOutput, calls=%fused_computation.20 | convolution fusion | flops 19330498560 | bytes 36175872 | tf_op jit(solution)/shard_map/tf,fd->td/dot_general | solution.py:29
  70.2 26.9 %fusion.14 = f32[4096,3072]{1,0:T(8,128)} fusion(bf16[4096,768]{1,0:T(8,128)(2,1)} %convolution_convert_fusion.1, bf16[2,768,3072]{2,1,0:T(8,128)(2,1)S(1)} %bitcast.63), kind=kOutput, calls=%fused_computation.23 | convolution fusion | flops 19327352832 | bytes 61341696 | tf_op jit(solution)/shard_map/td,df->tf/dot_general | solution.py:30
  97.2 43.2 %fusion.5 = bf16[4096,3072]{1,0:T(8,128)(2,1)} fusion(f32[4096,3072]{1,0:T(8,128)} %fusion.14, bf16[4096,768]{1,0:T(8,128)(2,1)} %param.13, bf16[2,3072,768]{2,1,0:T(8,128)(2,1)} %param.15), kind=kOutput, calls=%fused_computation.7 | convolution fusion | flops 19453181952 | bytes 86507520 | tf_op jit(solution)/shard_map/td,fd->tf/dot_general | solution.py:34
  140.4 25.1 %fusion.33 = f32[768,3072]{1,0:T(8,128)} fusion(bf16[4096,768]{1,0:T(8,128)(2,1)S(1)} %copy-done.10, bf16[4096,3072]{1,0:T(8,128)(2,1)} %fusion.5), kind=kOutput, calls=%fused_computation.52 | convolution fusion | flops 19327352832 | bytes 40894464 | tf_op jit(solution)/shard_map/td,tf->df/dot_general | solution.py:35
  165.6 26.0 %convolution_convert_fusion = bf16[4096,768]{1,0:T(8,128)(2,1)} fusion(bf16[4096,3072]{1,0:T(8,128)(2,1)} %fusion.5, bf16[2,768,3072]{2,1,0:T(8,128)(2,1)} %param.14), kind=kOutput, calls=%fused_computation.19 | convolution fusion | flops 19330498560 | bytes 36175872 | tf_op jit(solution)/shard_map/tf,df->td/dot_general | solution.py:36
  191.6 42.7 %fusion.11.clone.4 = bf16[4096,3072]{1,0:T(8,128)(2,1)} fusion(f32[4096,3072]{1,0:T(8,128)} %get-tuple-element.36, bf16[4096,768]{1,0:T(8,128)(2,1)} %convolution_convert_fusion, bf16[2,3072,768]{2,1,0:T(8,128)(2,1)} %param.15), kind=kOutput, calls=%fused_computation.13.clone.clone.clone.1 | convolution fusion | flops 19453181952 | bytes 86507520 | tf_op jit(solution)/shard_map/td,fd->tf/dot_general | solution.py:38
  234.3 25.6 %convolution_bitcast_fusion = f32[768,3072]{1,0:T(8,128)} fusion(bf16[4096,768]{1,0:T(8,128)(2,1)S(1)} %bitcast.65, bf16[4096,3072]{1,0:T(8,128)(2,1)} %fusion.11.clone.4), kind=kOutput, calls=%fused_computation.21 | convolution fusion | flops 19327352832 | bytes 40894464 | tf_op jit(solution)/shard_map/td,tf->df/dot_general | solution.py:39
  260.0 26.7 %fusion.34 = f32[3072,768]{1,0:T(8,128)} fusion(bf16[4096,3072]{1,0:T(8,128)(2,1)} %get-tuple-element.35, bf16[4096,768]{1,0:T(8,128)(2,1)} %convolution_convert_fusion), kind=kOutput, calls=%fused_computation.53 | convolution fusion | flops 19327352832 | bytes 40894464 | tf_op jit(solution)/shard_map/tf,td->fd/dot_general | solution.py:37
  286.8 29.1 %fusion.12 = f32[3072,768]{1,0:T(8,128)} fusion(bf16[4096,768]{1,0:T(8,128)(2,1)} %param.13, f32[4096,3072]{1,0:T(8,128)} %fusion.14), kind=kOutput, calls=%fused_computation.18 | convolution fusion | flops 19390267392 | bytes 66060288 | tf_op jit(solution)/shard_map/tf,td->fd/dot_general | solution.py:33
  318.0 2.1 multiply_reduce_fusion.1
  321.5 8.9 %reduce-scatter.5.cloned.1.call-done = f32[96,3072]{1,0:T(8,128)} async-done(((f32[768,3072]{1,0:T(8,128)}), f32[96,3072]{1,0:T(8,128)}) %reduce-scatter.5.cloned.1.call-update) | async-done | bytes 1179664 | tf_op jit(solution)/shard_map/reduce_scatter | solution.py:262
  331.8 2.5 pad_maximum_fusion
  334.3 67.0 %reduce-scatter.9.cloned.1.call-done = f32[384,768]{1,0:T(8,128)} async-done(((f32[3072,768]{1,0:T(8,128)}), f32[384,768]{1,0:T(8,128)}) %reduce-scatter.9.cloned.1.call-update) | async-done | bytes 1179664 | tf_op jit(solution)/shard_map/reduce_scatter | solution.py:262
  402.6 69.4 %reduce-scatter.11.cloned.1.call-done = f32[384,768]{1,0:T(8,128)} async-done(((f32[3072,768]{1,0:T(8,128)}), f32[384,768]{1,0:T(8,128)}) %reduce-scatter.11.cloned.1.call-update) | async-done | bytes 1179664 | tf_op jit(solution)/shard_map/reduce_scatter | solution.py:262
  473.4 2.5 pad_maximum_fusion.1
  477.8 6.0 stat_sum.1
  485.8 1.8 copy-done.2
  487.6 1.7 copy-done.3
  492.6 10.0 %moments.1 = (f32[2,96,3072]{2,1,0:T(8,128)}, f32[2,384,768]{2,1,0:T(8,128)}, f32[2,96,3072]{2,1,0:T(8,128)}, f32[2,384,768]{2,1,0:T(8,128)}, f32[2,96,3072]{2,1...) custom-call(f32[1]{0:T(128)} %bitcast.11.clip_ref, f32[2,96,3072]{2,1,0:T(8,128)S(1)} %copy-done.2, ...), custom_call_target="tpu_custom_call" | custom-call | tf_op jit(solution)/shard_map/moments/pallas_call | solution.py:126
  502.6 86.4 %update_and_gather.1 = (bf16[2,768,3072]{2,1,0:T(8,128)(2,1)}, bf16[2,3072,768]{2,1,0:T(8,128)(2,1)}, f32[2,96,3072]{2,1,0:T(8,128)S(1)}, f32[2,384,768]{2,1,0:T(8,128)S(1)}) custom-call(f32[1]{0:T(128)} %bitcast.61.rate_ref, f32[8,128]{1,0:T(8,128)S(1)} %broadcast_add_fusion.stats_ref, f32[2,96,3072]{2,1,0:T(8,128)S(1)} %get-tuple-element.21.u_up, ...), custom_call_target="tpu_custom_call" | custom-call | tf_op jit(solution)/shard_map/update_and_gather/pallas_call | solution.py:226
  591.8 8.3 %copy.29 = bf16[2,768,3072]{2,1,0:T(8,128)(2,1)} copy(bf16[2,768,3072]{2,1,0:T(8,128)(2,1)} %get-tuple-element.46) | data formatting | bytes 18874368
  600.1 8.2 %copy.30 = bf16[2,3072,768]{2,1,0:T(8,128)(2,1)} copy(bf16[2,3072,768]{2,1,0:T(8,128)(2,1)} %get-tuple-element.47) | data formatting | bytes 18874368
  608.2 3.3 copy.31
  (51 shorter events, 15.8 us)
Async XLA Ops:
  7.2 312.9 %reduce-scatter.7.cloned.1.call-start = ((), (), s32[]{:S(2)}) async-start(), calls=%async_computation.5 | async-start | bytes 10616832 | tf_op jit(solution)/shard_map/reduce_scatter | solution.py:262
  7.2 38.6 %copy-start.9 = (bf16[2,3072,768]{2,1,0:T(8,128)(2,1)S(1)}, bf16[2,3072,768]{2,1,0:T(8,128)(2,1)}, u32[]{:S(2)}) copy-start(bf16[2,3072,768]{2,1,0:T(8,128)(2,1)} %param.15) | copy-start | bytes 28311556
  7.2 63.0 %slice-start = ((s8[9437184]{0:T(1024)(128)(4,1)}), s8[4194304]{0:T(1024)(128)(4,1)S(1)}, s32[]{:S(2)}) async-start(s8[9437184]{0:T(1024)(128)(4,1)} %bitcast.62), calls=%async_computation.8 | async-start | bytes 8388608
  7.2 63.0 %slice-start.1 = ((s8[9437184]{0:T(1024)(128)(4,1)}), s8[4194304]{0:T(1024)(128)(4,1)S(1)}, s32[]{:S(2)}) async-start(s8[9437184]{0:T(1024)(128)(4,1)} %bitcast.62), calls=%async_computation.9 | async-start | bytes 8388608
  45.8 24.4 %slice-start.2 = ((s8[9437184]{0:T(1024)(128)(4,1)}), s8[1048576]{0:T(1024)(128)(4,1)S(1)}, s32[]{:S(2)}) async-start(s8[9437184]{0:T(1024)(128)(4,1)} %bitcast.62), calls=%async_computation.10 | async-start | bytes 2097152
  97.2 43.2 %copy-start.10 = (bf16[4096,768]{1,0:T(8,128)(2,1)S(1)}, bf16[4096,768]{1,0:T(8,128)(2,1)}, u32[]{:S(2)}) copy-start(bf16[4096,768]{1,0:T(8,128)(2,1)} %convolution_convert_fusion.1) | copy-start | bytes 18874372
  165.6 164.8 %reduce-scatter.5.cloned.1.call-start = ((), (), s32[]{:S(2)}) async-start(), calls=%async_computation.4 | async-start | bytes 10616832 | tf_op jit(solution)/shard_map/reduce_scatter | solution.py:262
  165.6 68.7 %slice-start.3 = ((s8[6291456]{0:T(1024)(128)(4,1)}), s8[4194304]{0:T(1024)(128)(4,1)S(1)}, s32[]{:S(2)}) async-start(s8[6291456]{0:T(1024)(128)(4,1)} %bitcast.64), calls=%async_computation.11 | async-start | bytes 8388608
  191.6 42.7 %slice-start.4 = ((s8[6291456]{0:T(1024)(128)(4,1)}), s8[2097152]{0:T(1024)(128)(4,1)S(1)}, s32[]{:S(2)}) async-start(s8[6291456]{0:T(1024)(128)(4,1)} %bitcast.64), calls=%async_computation.12 | async-start | bytes 4194304
  260.0 141.3 %reduce-scatter.9.cloned.1.call-start = ((), (), s32[]{:S(2)}) async-start(), calls=%async_computation.6 | async-start | bytes 10616832 | tf_op jit(solution)/shard_map/reduce_scatter | solution.py:262
  286.7 185.3 %reduce-scatter.11.cloned.1.call-start = ((), (), s32[]{:S(2)}) async-start(), calls=%async_computation.7 | async-start | bytes 10616832 | tf_op jit(solution)/shard_map/reduce_scatter | solution.py:262
  315.9 1.7 copy-start
  485.8 16.9 %copy-start.1 = (f32[2,96,3072]{2,1,0:T(8,128)S(1)}, f32[2,96,3072]{2,1,0:T(8,128)}, u32[]{:S(2)}) copy-start(f32[2,96,3072]{2,1,0:T(8,128)} %p_up.1) | copy-start | bytes 7077892
  485.8 1.8 copy-start.2
  487.6 1.7 copy-start.3
  489.3 1.7 copy-start.7
  490.9 1.7 copy-start.8
  589.0 1.4 copy-start.4
  590.4 1.4 copy-start.6
  600.1 11.5 %copy-start.5 = (f32[2,384,768]{2,1,0:T(8,128)S(1)}, f32[2,384,768]{2,1,0:T(8,128)}, u32[]{:S(2)}) copy-start(f32[2,384,768]{2,1,0:T(8,128)} %copy-done.4) | copy-start | bytes 7077892
Sparse Core Ops, SparseCore 0:
  165.7 70.2 reduce-scatter.6
  260.1 70.2 reduce-scatter.4
  333.8 67.4 reduce-scatter.8
  404.6 67.4 reduce-scatter.10

commit v2 on v1

--- a/solution.py
+++ b/solution.py
@@ -22,26 +22,7 @@
     return pre_act * normal_cdf, normal_cdf + pre_act * normal_pdf
 
 
-def local_grads(act_in, grad_out, w_up, w_down):
-    z_one = jnp.einsum("td,df->tf", act_in, w_up[0], preferred_element_type=jnp.float32)
-    gelu_one, slope_one = gelu_parts(z_one)
-    act_one = gelu_one.astype(jnp.bfloat16)
-    hidden = jnp.einsum("tf,fd->td", act_one, w_down[0], preferred_element_type=jnp.float32).astype(jnp.bfloat16)
-    z_three = jnp.einsum("td,df->tf", hidden, w_up[1], preferred_element_type=jnp.float32)
-    gelu_three, slope_three = gelu_parts(z_three)
-    act_three = gelu_three.astype(jnp.bfloat16)
-    g_four = jnp.einsum("tf,td->fd", act_three, grad_out, preferred_element_type=jnp.float32)
-    dz_three = (jnp.einsum("td,fd->tf", grad_out, w_down[1], preferred_element_type=jnp.float32) * slope_three).astype(jnp.bfloat16)
-    g_three = jnp.einsum("td,tf->df", hidden, dz_three, preferred_element_type=jnp.float32)
-    d_hidden = jnp.einsum("tf,df->td", dz_three, w_up[1], preferred_element_type=jnp.float32).astype(jnp.bfloat16)
-    g_two = jnp.einsum("tf,td->fd", act_one, d_hidden, preferred_element_type=jnp.float32)
-    dz_one = (jnp.einsum("td,fd->tf", d_hidden, w_down[0], preferred_element_type=jnp.float32) * slope_one).astype(jnp.bfloat16)
-    g_one = jnp.einsum("td,tf->df", act_in, dz_one, preferred_element_type=jnp.float32)
-    return g_one, g_two, g_three, g_four
-
-
 MESH = pl.DeviceIdType.MESH
-VMEM_LIMIT = 66 * 1024 * 1024 - 2 * 1024 * 1024
 
 
 def coords():
@@ -91,6 +72,466 @@
         compiler_params=pltpu.CompilerParams(collective_id=0, has_side_effects=True),
         name="stat_sum",
     )(tile)
+
+
+CHUNKS = 3
+LANES = 128
+TILE = 256
+OWNERS = tuple(chip * 2 + core for core in range(2) for chip in range(4))
+FULL_VMEM = 67043328
+
+
+def dot_nn(lhs, rhs):
+    return jnp.dot(lhs, rhs, preferred_element_type=jnp.float32)
+
+
+def dot_nt(lhs, rhs):
+    return lax.dot_general(lhs, rhs, (((1,), (1,)), ((), ())), preferred_element_type=jnp.float32)
+
+
+def dot_tn(lhs, rhs):
+    return lax.dot_general(lhs, rhs, (((0,), (0,)), ((), ())), preferred_element_type=jnp.float32)
+
+
+def chunk_blocks(chunk, width):
+    return [owner * width + chunk * LANES for owner in OWNERS]
+
+
+def forward_kernel(x_ref, w_up_ref, w_down_ref, a_out, s_out, h_out):
+    x = x_ref[...]
+    width = w_up_ref.shape[2] // len(OWNERS)
+    total = None
+    for chunk in range(CHUNKS):
+        starts = chunk_blocks(chunk, width)
+        w_in = jnp.concatenate([w_up_ref[0, :, s:s + LANES] for s in starts], axis=1)
+        gelu, slope = gelu_parts(dot_nn(x, w_in))
+        act = gelu.astype(jnp.bfloat16)
+        a_out[chunk] = act
+        s_out[chunk] = slope
+        w_out = jnp.concatenate([w_down_ref[0, s:s + LANES, :] for s in starts], axis=0)
+        part = dot_nn(act, w_out)
+        total = part if total is None else total + part
+    h_out[...] = total.astype(jnp.bfloat16)
+
+
+def forward_block(act_in, w_up, w_down, tile=512):
+    rows, dim = act_in.shape
+    ff = w_up.shape[2]
+    wide = ff // CHUNKS
+    return pl.pallas_call(
+        forward_kernel,
+        grid=(rows // tile,),
+        out_shape=[
+            jax.ShapeDtypeStruct((CHUNKS, rows, wide), jnp.bfloat16),
+            jax.ShapeDtypeStruct((CHUNKS, rows, wide), jnp.float32),
+            jax.ShapeDtypeStruct((rows, dim), jnp.bfloat16),
+        ],
+        in_specs=[
+            pl.BlockSpec((tile, dim), lambda i: (i, 0)),
+            pl.BlockSpec((1, dim, ff), lambda i: (0, 0, 0)),
+            pl.BlockSpec((1, ff, dim), lambda i: (0, 0, 0)),
+        ],
+        out_specs=[
+            pl.BlockSpec((CHUNKS, tile, wide), lambda i: (0, i, 0)),
+            pl.BlockSpec((CHUNKS, tile, wide), lambda i: (0, i, 0)),
+            pl.BlockSpec((tile, dim), lambda i: (i, 0)),
+        ],
+        compiler_params=pltpu.CompilerParams(dimension_semantics=("arbitrary",), vmem_limit_bytes=FULL_VMEM),
+        name="forward_block",
+    )(act_in, w_up, w_down)
+
+
+def backward_kernel(group_size, x_hbm, e_hbm, h_hbm, a_hbm, s_hbm, w_up_hbm, w_down_hbm,
+                    g1_out, g2_out, g3_out, g4_out, q_hbm,
+                    h_v, e_v, wu_v, wd_v, a_v, q_v, s_v, t_d, t_u,
+                    d0, d1a, d1b, d2a, d2b, u0, u1a, u1b, u2a, u2b,
+                    load_sem, w_sem, q_sem, s_sem, send_sem, recv_sem, free_sem):
+    me, partner, near_x, near_y = coords()
+    core, col, row = me % 2, (me // 2) % 2, me // 4
+    rows, dim = h_v.shape
+    half_rows = rows // 2
+    wide = wu_v.shape[2]
+    width = wide * CHUNKS // len(OWNERS)
+    tiles = half_rows // TILE
+    slots = s_v.shape[0]
+
+    def at_rows(start, size):
+        return pl.ds(pl.multiple_of(start, size), size)
+
+    def half_copy(src, dst, half, sem):
+        span = pl.ds(half * half_rows, half_rows)
+        return pltpu.make_async_copy(src.at[span], dst.at[span], load_sem.at[sem, half])
+
+    def start_weight(which, chunk, layer):
+        for j, start in enumerate(chunk_blocks(chunk, width)):
+            if which == 0:
+                pltpu.make_async_copy(w_up_hbm.at[layer, :, pl.ds(start, LANES)], wu_v.at[chunk, :, pl.ds(j * LANES, LANES)], w_sem.at[0, chunk]).start()
+            else:
+                pltpu.make_async_copy(w_down_hbm.at[layer, pl.ds(start, LANES), :], wd_v.at[chunk, pl.ds(j * LANES, LANES), :], w_sem.at[1, chunk]).start()
+
+    def wait_weight(which, chunk):
+        ref = (wu_v, wd_v)[which]
+        pltpu.make_async_copy(ref.at[chunk], ref.at[chunk], w_sem.at[which, chunk]).wait()
+
+    for half in range(2):
+        half_copy(h_hbm, h_v, half, 0).start()
+        half_copy(e_hbm, e_v, half, 1).start()
+        if half == 0:
+            start_weight(0, 0, 1)
+            start_weight(1, 0, 1)
+    for chunk in range(1, CHUNKS):
+        start_weight(0, chunk, 1)
+        start_weight(1, chunk, 1)
+    meet_all(me, group_size)
+
+    def hop(src, dst, kind, chunk, stage, device):
+        return remote(src, dst, send_sem.at[kind, chunk, stage], recv_sem.at[kind, chunk, stage], device)
+
+    def hop0(kind, i):
+        if kind == 0:
+            return hop(t_d.at[1 - core], d0.at[i], 0, i, 0, partner)
+        return hop(t_u.at[:, :, 1 - core], u0.at[i], 1, i, 0, partner)
+
+    def bufs(kind):
+        return (d0, d1a, d1b, d2a, d2b) if kind == 0 else (u0, u1a, u1b, u2a, u2b)
+
+    def hop1(kind, i):
+        b0, b1a, b1b, _, _ = bufs(kind)
+        cut = b1a.shape[3]
+        return (hop(b0.at[i, :, 1 - col, :, pl.ds(0, cut)], b1a.at[i], kind, i, 1, near_x),
+                hop(b0.at[i, 1 - row, :, :, pl.ds(cut, cut)], b1b.at[i], kind, i, 2, near_y))
+
+    def hop2(kind, i):
+        _, b1a, b1b, b2a, b2b = bufs(kind)
+        return (hop(b1a.at[i, 1 - row], b2a.at[i], kind, i, 3, near_y),
+                hop(b1b.at[i, 1 - col], b2b.at[i], kind, i, 4, near_x))
+
+    def rs0(kind, i):
+        hop0(kind, i).start()
+
+    def rs1(kind, i):
+        hop0(kind, i).wait()
+        b0 = bufs(kind)[0]
+        for y in range(2):
+            for x in range(2):
+                own = t_d[core, y, x] if kind == 0 else t_u[y, x, core]
+                b0[i, y, x] = b0[i, y, x] + own
+        for copy in hop1(kind, i):
+            copy.start()
+
+    def rs2(kind, i):
+        b0, b1a, b1b, _, _ = bufs(kind)
+        cut = b1a.shape[3]
+        first, second = hop1(kind, i)
+        out_a, out_b = hop2(kind, i)
+        first.wait()
+        for y in range(2):
+            b1a[i, y] = b1a[i, y] + b0[i, y, col, :, 0:cut]
+        out_a.start()
+        second.wait()
+        for x in range(2):
+            b1b[i, x] = b1b[i, x] + b0[i, row, x, :, cut:2 * cut]
+        out_b.start()
+
+    def rs3(kind, i, out):
+        _, b1a, b1b, b2a, b2b = bufs(kind)
+        cut = b1a.shape[3]
+        for copy in hop2(kind, i):
+            copy.wait()
+        left = (b1a[i, row] + b2a[i]) / group_size
+        right = (b1b[i, col] + b2b[i]) / group_size
+        if kind == 0:
+            span = at_rows(i * LANES, LANES)
+            out[span, 0:cut] = left
+            out[span, cut:2 * cut] = right
+        else:
+            for j, owner in enumerate(OWNERS):
+                part = (left, right)[j // 4]
+                lane = (j % 4) * LANES
+                out[:, pl.ds(pl.multiple_of(owner * width + i * LANES, LANES), LANES)] = part[:, lane:lane + LANES]
+
+    def give_free(i):
+        for device in (partner, near_x, near_y):
+            pl.semaphore_signal(free_sem.at[i], inc=1, device_id=(device,), device_id_type=MESH)
+
+    def grad_down(lhs_ref, rhs_ref, half, before_store=None):
+        def part(m, carry):
+            acc = dot_tn(lhs_ref[:, at_rows(m * (wide // 2), wide // 2)], rhs_ref[at_rows(half * half_rows, half_rows), :])
+            if before_store is not None:
+                before_store(m)
+            acc = acc.reshape(t_d.shape[1:])
+            t_d[m] = acc + jnp.where(half == 0, 0.0, t_d[m])
+            return carry
+        lax.fori_loop(0, 2, part, 0)
+
+    def grad_up(lhs_ref, rhs_ref, half):
+        def part(m, carry):
+            acc = dot_tn(lhs_ref[at_rows(half * half_rows, half_rows), at_rows(m * (dim // 2), dim // 2)], rhs_ref[...])
+            acc = acc.reshape(t_u.shape[1:])
+            t_u[m] = acc + jnp.where(half == 0, 0.0, t_u[m])
+            return carry
+        lax.fori_loop(0, 2, part, 0)
+
+    def q_copy(i, half):
+        return pltpu.make_async_copy(q_v, q_hbm.at[i, at_rows(half * half_rows, half_rows), :], q_sem.at[0])
+
+    def second_chunk(i, carry):
+        wait_weight(0, i)
+        wait_weight(1, i)
+
+        def second_half(half, carry):
+            @pl.when(i == 0)
+            def _():
+                span = at_rows(half * half_rows, half_rows)
+                pltpu.make_async_copy(h_hbm.at[span], h_v.at[span], load_sem.at[0, half]).wait()
+                pltpu.make_async_copy(e_hbm.at[span], e_v.at[span], load_sem.at[1, half]).wait()
+
+            @pl.when((i > 0) | (half > 0))
+            def _():
+                q_copy(i, half).wait()
+
+            def second_tile(t, carry):
+                span = at_rows(half * half_rows + t * TILE, TILE)
+                z = dot_nn(h_v[span, :], wu_v[i])
+                p = dot_nt(e_v[span, :], wd_v[i])
+                gelu, slope = gelu_parts(z)
+                here = at_rows(t * TILE, TILE)
+                a_v[here, :] = gelu.astype(jnp.bfloat16)
+                q_v[here, :] = (p * slope).astype(jnp.bfloat16)
+
+                @pl.when((t == tiles // 2) & (half == 0) & (i > 0))
+                def _():
+                    @pl.when(i > 1)
+                    def _():
+                        rs3(0, i - 2, g4_out)
+                        rs3(1, i - 2, g3_out)
+                        give_free(i - 2)
+                    rs1(0, i - 1)
+                    rs1(1, i - 1)
+                return carry
+
+            lax.fori_loop(0, tiles, second_tile, 0)
+            q_copy(i, half).start()
+
+            @pl.when((half == 1) & (i > 0))
+            def _():
+                rs2(0, i - 1)
+                rs2(1, i - 1)
+
+            grad_down(a_v, e_v, half)
+
+            @pl.when(half == 1)
+            def _():
+                rs0(0, i)
+
+            grad_up(h_v, q_v, half)
+
+            @pl.when(half == 1)
+            def _():
+                rs0(1, i)
+            return carry
+
+        lax.fori_loop(0, 2, second_half, 0)
+        return carry
+
+    lax.fori_loop(0, CHUNKS, second_chunk, 0)
+
+    q_copy(CHUNKS - 1, 1).wait()
+    for half in range(2):
+        half_copy(x_hbm, e_v, half, 1).start()
+    for chunk in range(CHUNKS):
+        start_weight(1, chunk, 0)
+    r_rows = half_rows // 4
+    staging = (a_v, q_v)
+
+    def r_load(slot, t):
+        for k in range(CHUNKS):
+            pltpu.make_async_copy(q_hbm.at[k, at_rows(t * r_rows, r_rows), :], staging[slot].at[pl.ds(k * r_rows, r_rows), :], load_sem.at[2, slot]).start()
+
+    def a_load(i, half):
+        return pltpu.make_async_copy(a_hbm.at[i, pl.ds(half * half_rows, half_rows), :], staging[half], load_sem.at[0, half])
+
+    for slot in range(2):
+        r_load(slot, slot)
+    r_steps = rows // r_rows // 2
+
+    def r_pair(t, carry):
+        for slot in range(2):
+            whole = staging[slot].at[pl.ds(0, CHUNKS * r_rows), :]
+            pltpu.make_async_copy(whole, whole, load_sem.at[2, slot]).wait()
+            acc = dot_nt(staging[slot][0:r_rows, :], wu_v[0])
+            for k in range(1, CHUNKS):
+                acc = acc + dot_nt(staging[slot][k * r_rows:(k + 1) * r_rows, :], wu_v[k])
+            h_v[at_rows((2 * t + slot) * r_rows, r_rows), :] = acc.astype(jnp.bfloat16)
+
+            @pl.when(t < r_steps - 1)
+            def _():
+                r_load(slot, 2 * t + 2 + slot)
+
+        @pl.when(t == 0)
+        def _():
+            rs3(0, CHUNKS - 2, g4_out)
+            rs3(1, CHUNKS - 2, g3_out)
+            give_free(CHUNKS - 2)
+            rs1(0, CHUNKS - 1)
+            rs1(1, CHUNKS - 1)
+        return carry
+
+    lax.fori_loop(0, r_steps, r_pair, 0)
+    for half in range(2):
+        a_load(0, half).start()
+
+    def s_load(i, t):
+        slot = lax.rem(t, slots)
+        return pltpu.make_async_copy(s_hbm.at[i, at_rows(t * TILE, TILE), :], s_v.at[slot], s_sem.at[slot])
+
+    for t in range(slots):
+        s_load(0, t).start()
+    rs2(0, CHUNKS - 1)
+    rs2(1, CHUNKS - 1)
+
+    def first_down(i, carry):
+        for half in range(2):
+            a_load(i, half).wait()
+
+            def settle(m):
+                @pl.when((m == 0) & (i > 0))
+                def _():
+                    rs1(0, i - 1)
+
+            grad_down(staging[half], h_v, half, settle if half == 0 else None)
+
+            @pl.when(i < CHUNKS - 1)
+            def _():
+                a_load(i + 1, half).start()
+
+            if half == 0:
+                @pl.when(i == 2)
+                def _():
+                    rs2(0, 0)
+
+        @pl.when(i == 1)
+        def _():
+            rs3(0, CHUNKS - 1, g4_out)
+            rs3(1, CHUNKS - 1, g3_out)
+            give_free(CHUNKS - 1)
+
+        pl.semaphore_wait(free_sem.at[i], 3)
+        rs0(0, i)
+        return carry
+
+    lax.fori_loop(0, CHUNKS, first_down, 0)
+    for half in range(2):
+        half_copy(x_hbm, e_v, half, 1).wait()
+
+    def first_up(i, carry):
+        wait_weight(1, i)
+
+        def first_half(half, carry):
+            def first_tile(t, carry):
+                tt = half * tiles + t
+                s_load(i, tt).wait()
+                p = dot_nt(h_v[at_rows(tt * TILE, TILE), :], wd_v[i])
+                q_v[at_rows(t * TILE, TILE), :] = (p * s_v[lax.rem(tt, slots)]).astype(jnp.bfloat16)
+
+                ahead = tt + slots
+                @pl.when(ahead < 2 * tiles)
+                def _():
+                    s_load(i, ahead).start()
+
+                @pl.when((t == tiles // 2) & (half == 0))
+                def _():
+                    @pl.when(i == 0)
+                    def _():
+                        rs1(0, 2)
+                        rs2(0, 1)
+                        rs3(0, 0, g2_out)
+
+                    @pl.when(i == 1)
+                    def _():
+                        rs1(1, 0)
+                        rs2(0, 2)
+                        rs3(0, 1, g2_out)
+
+                    @pl.when(i == 2)
+                    def _():
+                        rs1(1, 1)
+                        rs2(1, 0)
+                        rs3(0, 2, g2_out)
+                return carry
+
+            lax.fori_loop(0, tiles, first_tile, 0)
+
+            @pl.when((half == 1) & (i < CHUNKS - 1))
+            def _():
+                for t in range(slots):
+                    s_load(i + 1, t).start()
+
+            grad_up(e_v, q_v, half)
+            return carry
+
+        lax.fori_loop(0, 2, first_half, 0)
+        rs0(1, i)
+        return carry
+
+    lax.fori_loop(0, CHUNKS, first_up, 0)
+    rs2(1, 1)
+    rs1(1, 2)
+    rs3(1, 0, g1_out)
+    rs3(1, 1, g1_out)
+    rs2(1, 2)
+    rs3(1, 2, g1_out)
+
+
+def backward_blocks(group_size, act_in, grad_out, hidden, act_one, slope_one, w_up, w_down):
+    rows, dim = act_in.shape
+    ff = w_up.shape[2]
+    wide = ff // CHUNKS
+    up_rows, down_rows = dim // group_size, LANES
+    hbm = pl.BlockSpec(memory_space=pl.ANY)
+    vmem = pl.BlockSpec(memory_space=pltpu.VMEM)
+    f32 = jnp.float32
+    bf16 = jnp.bfloat16
+    up_grad = jax.ShapeDtypeStruct((up_rows, ff), f32)
+    down_grad = jax.ShapeDtypeStruct((ff // group_size, dim), f32)
+
+    def stages(height, cols):
+        return [
+            pltpu.VMEM((CHUNKS, 2, 2, height, cols), f32),
+            pltpu.VMEM((CHUNKS, 2, height, cols // 2), f32),
+            pltpu.VMEM((CHUNKS, 2, height, cols // 2), f32),
+            pltpu.VMEM((CHUNKS, height, cols // 2), f32),
+            pltpu.VMEM((CHUNKS, height, cols // 2), f32),
+        ]
+
+    return pl.pallas_call(
+        functools.partial(backward_kernel, group_size),
+        out_shape=[up_grad, down_grad, up_grad, down_grad, jax.ShapeDtypeStruct((CHUNKS, rows, wide), bf16)],
+        in_specs=[hbm] * 7,
+        out_specs=[vmem] * 4 + [hbm],
+        scratch_shapes=[
+            pltpu.VMEM((rows, dim), bf16),
+            pltpu.VMEM((rows, dim), bf16),
+            pltpu.VMEM((CHUNKS, dim, wide), bf16),
+            pltpu.VMEM((CHUNKS, wide, dim), bf16),
+            pltpu.VMEM((rows // 2, wide), bf16),
+            pltpu.VMEM((rows // 2, wide), bf16),
+            pltpu.VMEM((2, TILE, wide), f32),
+            pltpu.VMEM((2, 2, 2, down_rows, dim), f32),
+            pltpu.VMEM((2, 2, 2, up_rows, wide), f32),
+            *stages(down_rows, dim),
+            *stages(up_rows, wide),
+            pltpu.SemaphoreType.DMA((3, 2)),
+            pltpu.SemaphoreType.DMA((2, CHUNKS)),
+            pltpu.SemaphoreType.DMA((1,)),
+            pltpu.SemaphoreType.DMA((2,)),
+            pltpu.SemaphoreType.DMA((2, CHUNKS, 5)),
+            pltpu.SemaphoreType.DMA((2, CHUNKS, 5)),
+            pltpu.SemaphoreType.REGULAR((CHUNKS,)),
+        ],
+        compiler_params=pltpu.CompilerParams(collective_id=2, has_side_effects=True, vmem_limit_bytes=FULL_VMEM),
+        name="backward_blocks",
+    )(act_in, grad_out, hidden, act_one, slope_one, w_up, w_down)[:4]
 
 
 def moments_kernel(clip_ref, g_up, g_down, m_up, m_down, v_up, v_down, m_up_out, m_down_out, v_up_out, v_down_out, u_up, u_down, stats):
@@ -258,15 +699,9 @@
     state_rows = P(None, "data", None)
     replicated = P()
 
-    def reduce_rows(grad):
-        return lax.psum_scatter(grad, "data", scatter_dimension=0, tiled=True) / group_size
-
     def device_step(act_in, grad_out, w_up, w_down, master_up, master_down, exp_avg_up, exp_avg_down, exp_sq_up, exp_sq_down, learn_rate, clip_norm):
-        g_one, g_two, g_three, g_four = local_grads(act_in, grad_out, w_up, w_down)
-        shard_four = reduce_rows(g_four)
-        shard_three = reduce_rows(g_three)
-        shard_two = reduce_rows(g_two)
-        shard_one = reduce_rows(g_one)
+        act_one, slope_one, hidden = forward_block(act_in, w_up, w_down)
+        shard_one, shard_two, shard_three, shard_four = backward_blocks(group_size, act_in, grad_out, hidden, act_one, slope_one, w_up, w_down)
         grad_up = jnp.stack([shard_one, shard_three])
         grad_down = jnp.stack([shard_two, shard_four])
         local_sq = jnp.sum(grad_up * grad_up) + jnp.sum(grad_down * grad_down)

time: 629 us -> 481 us (0.76); the launches traced: 621 us -> 480 us
  Pallas kernels: 102 us -> 427 us
  matrix products: 308 us -> 0 us
  waiting for transfers between devices: 145 us -> 0 us
  between operations: 19 us -> 5.21 us
  local copies, waits for them, and re-layouts: 32.8 us -> 39.5 us
    pallas_call x0 -> x2, Pallas kernels: none -> 325 us  [the longest x1 269 us: backward_blocks(): pl.pallas_call(functools.partial(backward_kernel, group_size), out_shape=...]
    dot_general x10 -> x0, matrix products: 308 us -> none  [the longest x1 43.2 us: local_grads(): jnp.einsum('td,fd->tf', grad_out, w_down[1], preferred_element_type=jnp.f...]
    reduce_scatter x4 -> x0, waiting for transfers between devices: 145 us -> none  [reduce_rows(): lax.psum_scatter(grad, 'data', scatter_dimension=0, tiled=True) / group_size]
    unnamed x36 -> x38, local copies, waits for them, and re-layouts: 31 us -> 37.8 us
  transfers between devices with their start and end apart: 4 -> 0, of which waited for: 3 -> 0; matrix products, arithmetic and copies ran while one was open for 26% -> 0% of each run, Pallas kernels for 0% -> 0%
where the time goes in v2:
time: 481 us; the launch traced here: 480 us
  Pallas kernels  427 us (89%)
  local copies, waits for them, and re-layouts  39.5 us (8%)
  other arithmetic  7.81 us (2%)
  between operations  5.21 us (1%)
    pallas_call x1, Pallas kernels, backward_blocks(): pl.pallas_call(functools.partial(backward_kernel, group_size), out_shape=...  269 us
    pallas_call x1, Pallas kernels, update_and_gather(): pl.pallas_call(functools.partial(update_kernel, group_size), out_shape=[j...  86.4 us
    pallas_call x1, Pallas kernels, forward_block(): pl.pallas_call(forward_kernel, grid=(rows // tile,), out_shape=[jax.Shape...  56.2 us
    unnamed x38, local copies, waits for them, and re-layouts  37.8 us
    pallas_call x1, Pallas kernels, moments(): pl.pallas_call(moments_kernel, grid=(steps,), out_shape=[up_shape, down_s...  10.1 us

profile of v2, /device:TPU:0, one launch (start us, length us, event | category | flops | bytes accessed | tf_op | source)
XLA Modules:
  0.0 479.9 jit_solution(16279046953837885371)
XLA Ops:
  0.6 56.2 %forward_block.1 = (bf16[3,4096,1024]{2,1,0:T(8,128)(2,1)}, f32[3,4096,1024]{2,1,0:T(8,128)}, bf16[4096,768]{1,0:T(8,128)(2,1)}) custom-call(bf16[4096,768]{1,0:T(8,128)(2,1)} %x_hbm.1, bf16[2,768,3072]{2,1,0:T(8,128)(2,1)} %w_up_hbm.1, bf16[2,3072,768]{2,1,0:T(8,128)(2,1)} %w_down_hbm.1), custom_call_target="tpu_custom_call" | custom-call | tf_op jit(solution)/shard_map/forward_block/pallas_call | solution.py:121
  56.8 268.6 %backward_blocks.1 = (f32[96,3072]{1,0:T(8,128)}, f32[384,768]{1,0:T(8,128)}, f32[96,3072]{1,0:T(8,128)}, f32[384,768]{1,0:T(8,128)}, bf16[3,4096,1024]{2,1,0:T(8,128)(2,1)}) custom-call(bf16[4096,768]{1,0:T(8,128)(2,1)} %x_hbm.1, bf16[4096,768]{1,0:T(8,128)(2,1)} %e_hbm.1, bf16[4096,768]{1,0:T(8,128)(2,1)} %get-tuple-element.27.h_hbm, ...), custom_call_target="tpu_custom_call" | custom-call | tf_op jit(solution)/shard_map/backward_blocks/pallas_call | solution.py:507
  325.5 4.3 pad_maximum_fusion.1
  329.8 2.5 pad_maximum_fusion
  333.7 0.6 broadcast_in_dim.4.tile_ref
  334.3 6.0 %stat_sum.1 = f32[8,128]{1,0:T(8,128)} custom-call(f32[8,128]{1,0:T(8,128)} %broadcast_in_dim.4.tile_ref), custom_call_target="tpu_custom_call" | custom-call | tf_op jit(solution)/shard_map/stat_sum/pallas_call | solution.py:66
  340.3 1.2 slice.3
  342.9 1.7 copy-done.3
  344.6 1.7 copy-done.4
  346.2 1.7 copy-done.9
  347.9 1.7 copy-done.10
  349.6 10.1 %moments.1 = (f32[2,96,3072]{2,1,0:T(8,128)}, f32[2,384,768]{2,1,0:T(8,128)}, f32[2,96,3072]{2,1,0:T(8,128)}, f32[2,384,768]{2,1,0:T(8,128)}, f32[2,96,3072]{2,1...) custom-call(f32[1]{0:T(128)} %bitcast.6.clip_ref, f32[2,96,3072]{2,1,0:T(8,128)S(1)} %copy-done.4, ...), custom_call_target="tpu_custom_call" | custom-call | tf_op jit(solution)/shard_map/moments/pallas_call | solution.py:567
  360.1 2.9 copy-done.1
  364.2 1.7 copy-done.2
  365.9 1.7 copy-done.12
  367.6 1.7 copy-done.14
  369.2 86.4 %update_and_gather.1 = (bf16[2,768,3072]{2,1,0:T(8,128)(2,1)}, bf16[2,3072,768]{2,1,0:T(8,128)(2,1)}, f32[2,96,3072]{2,1,0:T(8,128)S(1)}, f32[2,384,768]{2,1,0:T(8,128)S(1)}) custom-call(f32[1]{0:T(128)} %bitcast.7.rate_ref, f32[8,128]{1,0:T(8,128)S(1)} %broadcast_add_fusion.stats_ref, f32[2,96,3072]{2,1,0:T(8,128)S(1)} %copy-done.12, ...), custom_call_target="tpu_custom_call" | custom-call | tf_op jit(solution)/shard_map/update_and_gather/pallas_call | solution.py:667
  455.6 1.4 copy-done.5
  457.0 1.4 copy-done.7
  458.4 8.3 %copy.27 = bf16[2,768,3072]{2,1,0:T(8,128)(2,1)} copy(bf16[2,768,3072]{2,1,0:T(8,128)(2,1)} %get-tuple-element.58) | data formatting | bytes 18874368
  466.7 8.2 %copy.28 = bf16[2,3072,768]{2,1,0:T(8,128)(2,1)} copy(bf16[2,3072,768]{2,1,0:T(8,128)(2,1)} %get-tuple-element.59) | data formatting | bytes 18874368
  474.8 1.4 copy.29
  476.2 1.1 copy-done.6
  477.4 1.4 copy.30
  (27 shorter events, 1.0 us)
Async XLA Ops:
  325.5 4.3 copy-start.15
  325.5 4.3 copy-start.16
  342.9 1.7 copy-start.3
  344.6 1.7 copy-start.4
  346.2 1.7 copy-start.9
  347.9 1.7 copy-start.10
  349.6 10.1 %copy-start = (f32[2,384,768]{2,1,0:T(8,128)S(1)}, f32[2,384,768]{2,1,0:T(8,128)}, u32[]{:S(2)}) copy-start(f32[2,384,768]{2,1,0:T(8,128)} %p_down.1) | copy-start | bytes 7077892
  359.6 3.8 copy-start.11
  359.6 3.8 copy-start.13
  359.7 3.4 copy-start.1
  364.2 1.7 copy-start.2
  365.9 1.7 copy-start.12
  367.6 1.7 copy-start.14
  455.6 1.4 copy-start.5
  457.0 1.4 copy-start.7
  466.7 8.2 %copy-start.8 = (f32[2,96,3072]{2,1,0:T(8,128)S(1)}, f32[2,96,3072]{2,1,0:T(8,128)}, u32[]{:S(2)}) copy-start(f32[2,96,3072]{2,1,0:T(8,128)} %copy-done.7) | copy-start | bytes 7077892
  474.8 2.5 copy-start.6

commit v3 on v2

--- a/solution.py
+++ b/solution.py
@@ -50,33 +50,10 @@
     return copies
 
 
-def stat_sum_kernel(group_size, tile_ref, out_ref, slots, send_sem, recv_sem):
-    me = lax.axis_index("data")
-    slots[me] = tile_ref[...]
-    meet_all(me, group_size)
-    for copy in exchange_start(me, group_size, slots, send_sem, recv_sem):
-        copy.wait()
-    total = slots[0]
-    for index in range(1, group_size):
-        total = total + slots[index]
-    out_ref[...] = total
-
-
-def stat_sum(tile, group_size):
-    return pl.pallas_call(
-        functools.partial(stat_sum_kernel, group_size),
-        out_shape=jax.ShapeDtypeStruct((8, 128), jnp.float32),
-        in_specs=[pl.BlockSpec(memory_space=pltpu.VMEM)],
-        out_specs=pl.BlockSpec(memory_space=pltpu.VMEM),
-        scratch_shapes=[pltpu.VMEM((group_size, 8, 128), jnp.float32), pltpu.SemaphoreType.DMA((group_size,)), pltpu.SemaphoreType.DMA((group_size,))],
-        compiler_params=pltpu.CompilerParams(collective_id=0, has_side_effects=True),
-        name="stat_sum",
-    )(tile)
-
-
 CHUNKS = 3
 LANES = 128
 TILE = 256
+SLOTS = 4
 OWNERS = tuple(chip * 2 + core for core in range(2) for chip in range(4))
 FULL_VMEM = 67043328
 
@@ -142,10 +119,10 @@
 
 
 def backward_kernel(group_size, x_hbm, e_hbm, h_hbm, a_hbm, s_hbm, w_up_hbm, w_down_hbm,
-                    g1_out, g2_out, g3_out, g4_out, q_hbm,
+                    g1_out, g2_out, g3_out, g4_out, norm_out, q_hbm,
                     h_v, e_v, wu_v, wd_v, a_v, q_v, s_v, t_d, t_u,
                     d0, d1a, d1b, d2a, d2b, u0, u1a, u1b, u2a, u2b,
-                    load_sem, w_sem, q_sem, s_sem, send_sem, recv_sem, free_sem):
+                    sq_v, slots_v, load_sem, w_sem, q_sem, s_sem, send_sem, recv_sem, free_sem, stat_send, stat_recv):
     me, partner, near_x, near_y = coords()
     core, col, row = me % 2, (me // 2) % 2, me // 4
     rows, dim = h_v.shape
@@ -173,15 +150,11 @@
         ref = (wu_v, wd_v)[which]
         pltpu.make_async_copy(ref.at[chunk], ref.at[chunk], w_sem.at[which, chunk]).wait()
 
-    for half in range(2):
-        half_copy(h_hbm, h_v, half, 0).start()
-        half_copy(e_hbm, e_v, half, 1).start()
-        if half == 0:
-            start_weight(0, 0, 1)
-            start_weight(1, 0, 1)
-    for chunk in range(1, CHUNKS):
-        start_weight(0, chunk, 1)
-        start_weight(1, chunk, 1)
+    half_copy(h_hbm, h_v, 0, 0).start()
+    start_weight(0, 0, 1)
+    half_copy(e_hbm, e_v, 0, 1).start()
+    start_weight(1, 0, 1)
+    sq_v[...] = jnp.zeros_like(sq_v)
     meet_all(me, group_size)
 
     def hop(src, dst, kind, chunk, stage, device):
@@ -240,6 +213,9 @@
             copy.wait()
         left = (b1a[i, row] + b2a[i]) / group_size
         right = (b1b[i, col] + b2b[i]) / group_size
+        square = (left * left + right * right).reshape(left.shape[0] // 8, 8, cut).sum(axis=0)
+        for lane in range(0, cut, LANES):
+            sq_v[...] += square[:, lane:lane + LANES]
         if kind == 0:
             span = at_rows(i * LANES, LANES)
             out[span, 0:cut] = left
@@ -279,12 +255,21 @@
         wait_weight(0, i)
         wait_weight(1, i)
 
+        @pl.when(i == 0)
+        def _():
+            half_copy(h_hbm, h_v, 0, 0).wait()
+            half_copy(e_hbm, e_v, 0, 1).wait()
+            half_copy(h_hbm, h_v, 1, 0).start()
+            half_copy(e_hbm, e_v, 1, 1).start()
+            for chunk in range(1, CHUNKS):
+                start_weight(0, chunk, 1)
+                start_weight(1, chunk, 1)
+
         def second_half(half, carry):
-            @pl.when(i == 0)
+            @pl.when((i == 0) & (half == 1))
             def _():
-                span = at_rows(half * half_rows, half_rows)
-                pltpu.make_async_copy(h_hbm.at[span], h_v.at[span], load_sem.at[0, half]).wait()
-                pltpu.make_async_copy(e_hbm.at[span], e_v.at[span], load_sem.at[1, half]).wait()
+                half_copy(h_hbm, h_v, 1, 0).wait()
+                half_copy(e_hbm, e_v, 1, 1).wait()
 
             @pl.when((i > 0) | (half > 0))
             def _():
@@ -313,16 +298,16 @@
             lax.fori_loop(0, tiles, second_tile, 0)
             q_copy(i, half).start()
 
+            grad_down(a_v, e_v, half)
+
+            @pl.when(half == 1)
+            def _():
+                rs0(0, i)
+
             @pl.when((half == 1) & (i > 0))
             def _():
                 rs2(0, i - 1)
                 rs2(1, i - 1)
-
-            grad_down(a_v, e_v, half)
-
-            @pl.when(half == 1)
-            def _():
-                rs0(0, i)
 
             grad_up(h_v, q_v, half)
 
@@ -359,10 +344,12 @@
         for slot in range(2):
             whole = staging[slot].at[pl.ds(0, CHUNKS * r_rows), :]
             pltpu.make_async_copy(whole, whole, load_sem.at[2, slot]).wait()
-            acc = dot_nt(staging[slot][0:r_rows, :], wu_v[0])
-            for k in range(1, CHUNKS):
-                acc = acc + dot_nt(staging[slot][k * r_rows:(k + 1) * r_rows, :], wu_v[k])
-            h_v[at_rows((2 * t + slot) * r_rows, r_rows), :] = acc.astype(jnp.bfloat16)
+            for part in range(2):
+                m = part * (r_rows // 2)
+                acc = dot_nt(staging[slot][m:m + r_rows // 2, :], wu_v[0])
+                for k in range(1, CHUNKS):
+                    acc = acc + dot_nt(staging[slot][k * r_rows + m:k * r_rows + m + r_rows // 2, :], wu_v[k])
+                h_v[at_rows((2 * t + slot) * r_rows + m, r_rows // 2), :] = acc.astype(jnp.bfloat16)
 
             @pl.when(t < r_steps - 1)
             def _():
@@ -481,6 +468,13 @@
     rs3(1, 1, g1_out)
     rs2(1, 2)
     rs3(1, 2, g1_out)
+    slots_v[me] = sq_v[...]
+    for copy in exchange_start(me, group_size, slots_v, stat_send, stat_recv):
+        copy.wait()
+    total = slots_v[0]
+    for index in range(1, group_size):
+        total = total + slots_v[index]
+    norm_out[...] = jnp.full(norm_out.shape, jnp.sum(total))
 
 
 def backward_blocks(group_size, act_in, grad_out, hidden, act_one, slope_one, w_up, w_down):
@@ -506,9 +500,9 @@
 
     return pl.pallas_call(
         functools.partial(backward_kernel, group_size),
-        out_shape=[up_grad, down_grad, up_grad, down_grad, jax.ShapeDtypeStruct((CHUNKS, rows, wide), bf16)],
+        out_shape=[up_grad, down_grad, up_grad, down_grad, jax.ShapeDtypeStruct((8, 128), f32), jax.ShapeDtypeStruct((CHUNKS, rows, wide), bf16)],
         in_specs=[hbm] * 7,
-        out_specs=[vmem] * 4 + [hbm],
+        out_specs=[vmem] * 5 + [hbm],
         scratch_shapes=[
             pltpu.VMEM((rows, dim), bf16),
             pltpu.VMEM((rows, dim), bf16),
@@ -516,33 +510,37 @@
             pltpu.VMEM((CHUNKS, wide, dim), bf16),
             pltpu.VMEM((rows // 2, wide), bf16),
             pltpu.VMEM((rows // 2, wide), bf16),
-            pltpu.VMEM((2, TILE, wide), f32),
+            pltpu.VMEM((SLOTS, TILE, wide), f32),
             pltpu.VMEM((2, 2, 2, down_rows, dim), f32),
             pltpu.VMEM((2, 2, 2, up_rows, wide), f32),
             *stages(down_rows, dim),
             *stages(up_rows, wide),
+            pltpu.VMEM((8, 128), f32),
+            pltpu.VMEM((group_size, 8, 128), f32),
             pltpu.SemaphoreType.DMA((3, 2)),
             pltpu.SemaphoreType.DMA((2, CHUNKS)),
             pltpu.SemaphoreType.DMA((1,)),
-            pltpu.SemaphoreType.DMA((2,)),
+            pltpu.SemaphoreType.DMA((SLOTS,)),
             pltpu.SemaphoreType.DMA((2, CHUNKS, 5)),
             pltpu.SemaphoreType.DMA((2, CHUNKS, 5)),
             pltpu.SemaphoreType.REGULAR((CHUNKS,)),
+            pltpu.SemaphoreType.DMA((group_size,)),
+            pltpu.SemaphoreType.DMA((group_size,)),
         ],
         compiler_params=pltpu.CompilerParams(collective_id=2, has_side_effects=True, vmem_limit_bytes=FULL_VMEM),
         name="backward_blocks",
-    )(act_in, grad_out, hidden, act_one, slope_one, w_up, w_down)[:4]
-
-
-def moments_kernel(clip_ref, g_up, g_down, m_up, m_down, v_up, v_down, m_up_out, m_down_out, v_up_out, v_down_out, u_up, u_down, stats):
+    )(act_in, grad_out, hidden, act_one, slope_one, w_up, w_down)[:5]
+
+
+def moments_kernel(clip_ref, norm_ref, g_one, g_two, g_three, g_four, m_up, m_down, v_up, v_down, m_up_out, m_down_out, v_up_out, v_down_out, u_up, u_down, stats):
     bias_one = 1.0 - BETA_ONE ** STEP
     bias_two = 1.0 - BETA_TWO ** STEP
-    scale = clip_ref[0]
+    scale = jnp.minimum(1.0, clip_ref[0] / (jnp.sqrt(norm_ref[0:1, 0:1]) + NORM_EPS))
     row_id = lax.broadcasted_iota(jnp.int32, (8, 128), 0)
     sums = jnp.zeros((8, 128), jnp.float32)
-    for family, (g, m, v, m_out, v_out, u) in enumerate([(g_up, m_up, v_up, m_up_out, v_up_out, u_up), (g_down, m_down, v_down, m_down_out, v_down_out, u_down)]):
+    for family, (grads, m, v, m_out, v_out, u) in enumerate([((g_one, g_three), m_up, v_up, m_up_out, v_up_out, u_up), ((g_two, g_four), m_down, v_down, m_down_out, v_down_out, u_down)]):
         for layer in range(2):
-            grad = g[layer]
+            grad = grads[layer][...]
             avg_new = BETA_ONE * m[layer] + (1.0 - BETA_ONE) * scale * grad
             sq_new = BETA_TWO * v[layer] + (1.0 - BETA_TWO) * (scale * scale) * (grad * grad)
             direction = (avg_new / bias_one) / (jnp.sqrt(sq_new / bias_two) + ADAM_EPS)
@@ -558,30 +556,45 @@
     stats[...] += sums
 
 
-def moments(clip_scale, g_up, g_down, m_up, m_down, v_up, v_down, steps=4):
-    up, down = g_up.shape, g_down.shape
+def moments(clip_norm, norm_tile, grads, m_up, m_down, v_up, v_down, steps=4):
+    up, down = m_up.shape, m_down.shape
     up_spec = pl.BlockSpec((2, up[1] // steps, up[2]), lambda i: (0, i, 0))
     down_spec = pl.BlockSpec((2, down[1] // steps, down[2]), lambda i: (0, i, 0))
+    up_grad = pl.BlockSpec((up[1] // steps, up[2]), lambda i: (i, 0))
+    down_grad = pl.BlockSpec((down[1] // steps, down[2]), lambda i: (i, 0))
+    tile = pl.BlockSpec((8, 128), lambda i: (0, 0))
     pair = [up_spec, down_spec]
     up_shape, down_shape = jax.ShapeDtypeStruct(up, jnp.float32), jax.ShapeDtypeStruct(down, jnp.float32)
     return pl.pallas_call(
         moments_kernel,
         grid=(steps,),
         out_shape=[up_shape, down_shape] * 3 + [jax.ShapeDtypeStruct((8, 128), jnp.float32)],
-        in_specs=[pl.BlockSpec(memory_space=pltpu.SMEM)] + pair * 3,
-        out_specs=pair * 3 + [pl.BlockSpec((8, 128), lambda i: (0, 0))],
-        compiler_params=pltpu.CompilerParams(dimension_semantics=("arbitrary",), vmem_limit_bytes=40 * 1024 * 1024),
+        in_specs=[pl.BlockSpec(memory_space=pltpu.SMEM), tile] + [up_grad, down_grad] * 2 + pair * 2,
+        out_specs=pair * 3 + [tile],
+        compiler_params=pltpu.CompilerParams(dimension_semantics=("arbitrary",), vmem_limit_bytes=FULL_VMEM),
         name="moments",
-    )(clip_scale.reshape(1), g_up, g_down, m_up, m_down, v_up, v_down)
+    )(clip_norm.reshape(1), norm_tile, *grads, m_up, m_down, v_up, v_down)
 
 
 PIECES = ((0, 0), (0, 1), (1, 0), (1, 1))
 
 
-def update_kernel(group_size, rate_ref, stats_ref, u_up, u_down, p_up, p_down, all_up, all_down, p_up_out, p_down_out,
-                  slots, w_up, w_down, stat_send, stat_recv, send_sem, recv_sem, local_sem):
+def update_kernel(group_size, rate_ref, stats_ref, u_up_hbm, u_down_hbm, p_up_hbm, p_down_hbm, all_up, all_down, p_up_out, p_down_out,
+                  slots, u_up, u_down, p_up, p_down, w_up, w_down, stat_send, stat_recv, send_sem, recv_sem, local_sem, in_sem, out_sem):
     me, partner, near_x, near_y = coords()
-    slots[me] = stats_ref[...]
+    loads = []
+    for src, dst in ((p_up_hbm, p_up), (p_down_hbm, p_down), (u_up_hbm, u_up), (u_down_hbm, u_down)):
+        for layer in range(2):
+            copy = pltpu.make_async_copy(src.at[layer], dst.at[layer], in_sem.at[len(loads)])
+            copy.start()
+            loads.append(copy)
+    row_id = lax.broadcasted_iota(jnp.int32, (8, 128), 0)
+    stats = stats_ref[...]
+    for index in range(4):
+        loads[index].wait()
+        master = (p_up, p_down)[index // 2][index % 2]
+        stats = stats + jnp.where(row_id == index, jnp.sum(master * master), 0.0)
+    slots[me] = stats
     meet_all(me, group_size)
     for copy in exchange_start(me, group_size, slots, stat_send, stat_recv):
         copy.wait()
@@ -618,8 +631,8 @@
         family, layer = PIECES[piece]
         u, p, p_out, w, full = params[family]
         index = 2 * family + layer
+        loads[4 + index].wait()
         new = p[layer] - rate * ratio[index:index + 1, 0:1] * u[layer]
-        p_out[layer] = new
         w[layer] = new.astype(jnp.bfloat16)
         own[piece] = w.at[layer]
         if family == 0:
@@ -628,6 +641,10 @@
             forward(own[piece], piece, me, near_y, 4)
         forward(own[piece], piece, me, partner, 1)
         copy = pltpu.make_async_copy(own[piece], place(piece, me), local_sem.at[piece])
+        copy.start()
+        local.append(copy)
+        p[layer] = new
+        copy = pltpu.make_async_copy(p.at[layer], p_out.at[layer], out_sem.at[piece])
         copy.start()
         local.append(copy)
     for piece in (2, 3):
@@ -672,10 +689,14 @@
             jax.ShapeDtypeStruct(up, jnp.float32),
             jax.ShapeDtypeStruct(down, jnp.float32),
         ],
-        in_specs=[pl.BlockSpec(memory_space=pltpu.SMEM)] + [vmem] * 5,
-        out_specs=[hbm, hbm, vmem, vmem],
+        in_specs=[pl.BlockSpec(memory_space=pltpu.SMEM), vmem] + [hbm] * 4,
+        out_specs=[hbm] * 4,
         scratch_shapes=[
             pltpu.VMEM((group_size, 8, 128), jnp.float32),
+            pltpu.VMEM(up, jnp.float32),
+            pltpu.VMEM(down, jnp.float32),
+            pltpu.VMEM(up, jnp.float32),
+            pltpu.VMEM(down, jnp.float32),
             pltpu.VMEM(up, jnp.bfloat16),
             pltpu.VMEM(down, jnp.bfloat16),
             pltpu.SemaphoreType.DMA((group_size,)),
@@ -683,14 +704,12 @@
             pltpu.SemaphoreType.DMA((32,)),
             pltpu.SemaphoreType.DMA((group_size, 4)),
             pltpu.SemaphoreType.DMA((4,)),
+            pltpu.SemaphoreType.DMA((8,)),
+            pltpu.SemaphoreType.DMA((4,)),
         ],
-        compiler_params=pltpu.CompilerParams(collective_id=1, has_side_effects=True, vmem_limit_bytes=40 * 1024 * 1024),
+        compiler_params=pltpu.CompilerParams(collective_id=1, has_side_effects=True, vmem_limit_bytes=FULL_VMEM),
         name="update_and_gather",
     )(learn_rate.reshape(1), stats, u_up, u_down, p_up, p_down)
-
-
-def sum_squares(stacked):
-    return jnp.sum(stacked * stacked, axis=(1, 2))
 
 
 def solution(mesh):
@@ -701,15 +720,9 @@
 
     def device_step(act_in, grad_out, w_up, w_down, master_up, master_down, exp_avg_up, exp_avg_down, exp_sq_up, exp_sq_down, learn_rate, clip_norm):
         act_one, slope_one, hidden = forward_block(act_in, w_up, w_down)
-        shard_one, shard_two, shard_three, shard_four = backward_blocks(group_size, act_in, grad_out, hidden, act_one, slope_one, w_up, w_down)
-        grad_up = jnp.stack([shard_one, shard_three])
-        grad_down = jnp.stack([shard_two, shard_four])
-        local_sq = jnp.sum(grad_up * grad_up) + jnp.sum(grad_down * grad_down)
-        grad_norm = jnp.sqrt(stat_sum(jnp.full((8, 128), local_sq), group_size)[0, 0])
-        clip_scale = jnp.minimum(1.0, clip_norm / (grad_norm + NORM_EPS))
-        master_sq = jnp.concatenate([sum_squares(master_up), sum_squares(master_down)])
-        avg_up, avg_down, sq_up, sq_down, dir_up, dir_down, dir_stats = moments(clip_scale, grad_up, grad_down, exp_avg_up, exp_avg_down, exp_sq_up, exp_sq_down)
-        stats = dir_stats + jnp.pad(master_sq, (0, 4))[:, None]
+        *grads, norm_tile = backward_blocks(group_size, act_in, grad_out, hidden, act_one, slope_one, w_up, w_down)
+        grad_norm = jnp.sqrt(norm_tile[0, 0])
+        avg_up, avg_down, sq_up, sq_down, dir_up, dir_down, stats = moments(clip_norm, norm_tile, grads, exp_avg_up, exp_avg_down, exp_sq_up, exp_sq_down)
         new_w_up, new_w_down, master_up_out, master_down_out = update_and_gather(group_size, learn_rate, stats, dir_up, dir_down, master_up, master_down)
         return (new_w_up, new_w_down, master_up_out, master_down_out, avg_up, avg_down, sq_up, sq_down, grad_norm)
 

time: 481 us -> 430 us (0.89)
  Pallas kernels: 427 us -> 405 us
  local copies, waits for them, and re-layouts: 39.5 us -> 21.6 us
  other arithmetic: 7.81 us -> 0 us
    pallas_call x1, Pallas kernels: 269 us -> 245 us  [backward_blocks(): pl.pallas_call(functools.partial(backward_kernel, group_size), out_shape=...]
    unnamed x38 -> x8, local copies, waits for them, and re-layouts: 37.8 us -> 20.4 us
    another operation x2 -> x0, other arithmetic: 6.86 us -> none  [the longest x1 4.32 us: device_step(): grad_down = jnp.stack([shard_two, shard_four])]
    pallas_call x1 -> x0, Pallas kernels: 6.04 us -> none  [stat_sum(): pl.pallas_call(functools.partial(stat_sum_kernel, group_size), out_shape=...]
where the time goes in v3:
time: 430 us
  Pallas kernels  405 us (94%)
  local copies, waits for them, and re-layouts  21.6 us (5%)
    pallas_call x1, Pallas kernels, backward_blocks(): pl.pallas_call(functools.partial(backward_kernel, group_size), out_shape=...  245 us
    pallas_call x1, Pallas kernels, update_and_gather(): pl.pallas_call(functools.partial(update_kernel, group_size), out_shape=[j...  89.5 us
    pallas_call x1, Pallas kernels, forward_block(): pl.pallas_call(forward_kernel, grid=(rows // tile,), out_shape=[jax.Shape...  56.2 us
    unnamed x8, local copies, waits for them, and re-layouts  20.4 us
    pallas_call x1, Pallas kernels, moments(): pl.pallas_call(moments_kernel, grid=(steps,), out_shape=[up_shape, down_s...  13.8 us

profile of v3, /device:TPU:0, one launch (start us, length us, event | category | flops | bytes accessed | tf_op | source)
XLA Modules:
  0.0 429.9 jit_solution(7486256559255606572)
XLA Ops:
  0.6 56.2 %forward_block.1 = (bf16[3,4096,1024]{2,1,0:T(8,128)(2,1)}, f32[3,4096,1024]{2,1,0:T(8,128)}, bf16[4096,768]{1,0:T(8,128)(2,1)}) custom-call(bf16[4096,768]{1,0:T(8,128)(2,1)} %x_hbm.1, bf16[2,768,3072]{2,1,0:T(8,128)(2,1)} %w_up_hbm.1, bf16[2,3072,768]{2,1,0:T(8,128)(2,1)} %w_down_hbm.1), custom_call_target="tpu_custom_call" | custom-call | tf_op jit(solution)/shard_map/forward_block/pallas_call | solution.py:98
  56.8 245.2 %backward_blocks.1 = (f32[96,3072]{1,0:T(8,128)}, f32[384,768]{1,0:T(8,128)}, f32[96,3072]{1,0:T(8,128)}, f32[384,768]{1,0:T(8,128)}, f32[8,128]{1,0:T(8,128)}, /*index=5*/bf16[3,4096,1024]{2,1,0:T(8,128)(2,1)}) custom-call(bf16[4096,768]{1,0:T(8,128)(2,1)} %x_hbm.1, bf16[4096,768]{1,0:T(8,128)(2,1)} %e_hbm.1, bf16[4096,768]{1,0:T(8,128)(2,1)} %get-tuple-element.28.h_hbm, ...), custom_call_target="tpu_custom_call" | custom-call | tf_op jit(solution)/shard_map/backward_blocks/pallas_call | solution.py:501
  302.7 13.8 %moments.1 = (f32[2,96,3072]{2,1,0:T(8,128)}, f32[2,384,768]{2,1,0:T(8,128)}, f32[2,96,3072]{2,1,0:T(8,128)}, f32[2,384,768]{2,1,0:T(8,128)}, f32[2,96,3072]{2,1...) custom-call(f32[1]{0:T(128)} %bitcast.4.clip_ref, f32[8,128]{1,0:T(8,128)} %get-tuple-element.31.norm_ref, ...), custom_call_target="tpu_custom_call" | custom-call | tf_op jit(solution)/shard_map/moments/pallas_call | solution.py:568
  317.1 89.5 %update_and_gather.1 = (bf16[2,768,3072]{2,1,0:T(8,128)(2,1)}, bf16[2,3072,768]{2,1,0:T(8,128)(2,1)}, f32[2,96,3072]{2,1,0:T(8,128)}, f32[2,384,768]{2,1,0:T(8,128)}) custom-call(f32[1]{0:T(128)} %bitcast.3.rate_ref, f32[8,128]{1,0:T(8,128)} %get-tuple-element.36.stats_ref, f32[2,96,3072]{2,1,0:T(8,128)} %get-tuple-element.37.u_up_hbm, ...), custom_call_target="tpu_custom_call" | custom-call | tf_op jit(solution)/shard_map/update_and_gather/pallas_call | solution.py:684
  406.5 1.2 slice.3
  408.4 8.3 %copy.27 = bf16[2,768,3072]{2,1,0:T(8,128)(2,1)} copy(bf16[2,768,3072]{2,1,0:T(8,128)(2,1)} %get-tuple-element.56) | data formatting | bytes 18874368
  416.7 0.0 copy-start.1
  416.7 8.2 %copy.28 = bf16[2,3072,768]{2,1,0:T(8,128)(2,1)} copy(bf16[2,3072,768]{2,1,0:T(8,128)(2,1)} %get-tuple-element.57) | data formatting | bytes 18874368
  424.9 0.0 copy-done.1
  424.9 0.0 copy-start
  424.9 1.4 copy.29
  426.3 1.1 copy-done
  427.4 1.4 copy.30
Async XLA Ops:
  416.7 8.2 %copy-start.1 = (f32[2,96,3072]{2,1,0:T(8,128)S(1)}, f32[2,96,3072]{2,1,0:T(8,128)}, u32[]{:S(2)}) copy-start(f32[2,96,3072]{2,1,0:T(8,128)} %get-tuple-element.58) | copy-start | bytes 7077892
  424.9 2.5 copy-start

commit v4 on v3

--- a/solution.py
+++ b/solution.py
@@ -230,11 +230,9 @@
         for device in (partner, near_x, near_y):
             pl.semaphore_signal(free_sem.at[i], inc=1, device_id=(device,), device_id_type=MESH)
 
-    def grad_down(lhs_ref, rhs_ref, half, before_store=None):
+    def grad_down(lhs_ref, rhs_ref, half):
         def part(m, carry):
             acc = dot_tn(lhs_ref[:, at_rows(m * (wide // 2), wide // 2)], rhs_ref[at_rows(half * half_rows, half_rows), :])
-            if before_store is not None:
-                before_store(m)
             acc = acc.reshape(t_d.shape[1:])
             t_d[m] = acc + jnp.where(half == 0, 0.0, t_d[m])
             return carry
@@ -284,30 +282,42 @@
                 a_v[here, :] = gelu.astype(jnp.bfloat16)
                 q_v[here, :] = (p * slope).astype(jnp.bfloat16)
 
-                @pl.when((t == tiles // 2) & (half == 0) & (i > 0))
-                def _():
-                    @pl.when(i > 1)
+                @pl.when((half == 0) & (i > 1))
+                def _():
+                    @pl.when(t == 0)
+                    def _():
+                        rs2(1, i - 2)
+
+                    @pl.when(t == 2)
                     def _():
                         rs3(0, i - 2, g4_out)
-                        rs3(1, i - 2, g3_out)
-                        give_free(i - 2)
+
+                @pl.when((t == tiles // 2) & (half == 0) & (i > 0))
+                def _():
                     rs1(0, i - 1)
-                    rs1(1, i - 1)
+
+                @pl.when((t == 3) & (half == 1) & (i > 0))
+                def _():
+                    rs2(0, i - 1)
                 return carry
 
             lax.fori_loop(0, tiles, second_tile, 0)
             q_copy(i, half).start()
 
+            @pl.when((half == 0) & (i > 1))
+            def _():
+                rs3(1, i - 2, g3_out)
+                give_free(i - 2)
+
             grad_down(a_v, e_v, half)
 
             @pl.when(half == 1)
             def _():
                 rs0(0, i)
 
-            @pl.when((half == 1) & (i > 0))
-            def _():
-                rs2(0, i - 1)
-                rs2(1, i - 1)
+            @pl.when((half == 0) & (i > 0))
+            def _():
+                rs1(1, i - 1)
 
             grad_up(h_v, q_v, half)
 
@@ -357,13 +367,17 @@
 
         @pl.when(t == 0)
         def _():
+            rs1(0, CHUNKS - 1)
             rs3(0, CHUNKS - 2, g4_out)
+
+        @pl.when(t == 1)
+        def _():
+            rs1(1, CHUNKS - 1)
             rs3(1, CHUNKS - 2, g3_out)
             give_free(CHUNKS - 2)
-            rs1(0, CHUNKS - 1)
-            rs1(1, CHUNKS - 1)
         return carry
 
+    rs2(1, CHUNKS - 2)
     lax.fori_loop(0, r_steps, r_pair, 0)
     for half in range(2):
         a_load(0, half).start()
@@ -375,44 +389,29 @@
     for t in range(slots):
         s_load(0, t).start()
     rs2(0, CHUNKS - 1)
-    rs2(1, CHUNKS - 1)
-
-    def first_down(i, carry):
-        for half in range(2):
-            a_load(i, half).wait()
-
-            def settle(m):
-                @pl.when((m == 0) & (i > 0))
-                def _():
-                    rs1(0, i - 1)
-
-            grad_down(staging[half], h_v, half, settle if half == 0 else None)
-
-            @pl.when(i < CHUNKS - 1)
-            def _():
-                a_load(i + 1, half).start()
-
-            if half == 0:
-                @pl.when(i == 2)
-                def _():
-                    rs2(0, 0)
-
-        @pl.when(i == 1)
+
+    def first_chunk(i, carry):
+        a_load(i, 0).wait()
+        grad_down(a_v, h_v, 0)
+
+        @pl.when(i < CHUNKS - 1)
         def _():
-            rs3(0, CHUNKS - 1, g4_out)
-            rs3(1, CHUNKS - 1, g3_out)
-            give_free(CHUNKS - 1)
-
+            a_load(i + 1, 0).start()
+
+        @pl.when(i == 2)
+        def _():
+            rs2(1, 0)
+
+        a_load(i, 1).wait()
+        grad_down(q_v, h_v, 1)
         pl.semaphore_wait(free_sem.at[i], 3)
         rs0(0, i)
-        return carry
-
-    lax.fori_loop(0, CHUNKS, first_down, 0)
-    for half in range(2):
-        half_copy(x_hbm, e_v, half, 1).wait()
-
-    def first_up(i, carry):
         wait_weight(1, i)
+
+        @pl.when(i == 0)
+        def _():
+            for half in range(2):
+                half_copy(x_hbm, e_v, half, 1).wait()
 
         def first_half(half, carry):
             def first_tile(t, carry):
@@ -426,26 +425,45 @@
                 def _():
                     s_load(i, ahead).start()
 
-                @pl.when((t == tiles // 2) & (half == 0))
-                def _():
-                    @pl.when(i == 0)
-                    def _():
-                        rs1(0, 2)
-                        rs2(0, 1)
-                        rs3(0, 0, g2_out)
-
-                    @pl.when(i == 1)
-                    def _():
-                        rs1(1, 0)
-                        rs2(0, 2)
-                        rs3(0, 1, g2_out)
-
-                    @pl.when(i == 2)
-                    def _():
-                        rs1(1, 1)
-                        rs2(1, 0)
-                        rs3(0, 2, g2_out)
+                @pl.when((tt == 6) & (i == 0))
+                def _():
+                    rs3(0, 2, g4_out)
+
+                @pl.when((tt == tiles + 3) & (i == 2))
+                def _():
+                    rs3(1, 0, g1_out)
                 return carry
+
+            @pl.when(half == 0)
+            def _():
+                @pl.when(i == 0)
+                def _():
+                    rs2(1, 2)
+
+                @pl.when(i == 1)
+                def _():
+                    rs2(0, 0)
+
+                @pl.when(i > 0)
+                def _():
+                    rs1(1, i - 1)
+
+            @pl.when(half == 1)
+            def _():
+                @pl.when(i == 2)
+                def _():
+                    rs2(0, 1)
+
+                rs1(0, i)
+
+                @pl.when(i == 0)
+                def _():
+                    rs3(1, 2, g3_out)
+                    give_free(2)
+
+                @pl.when(i == 1)
+                def _():
+                    rs3(0, 0, g2_out)
 
             lax.fori_loop(0, tiles, first_tile, 0)
 
@@ -459,14 +477,20 @@
 
         lax.fori_loop(0, 2, first_half, 0)
         rs0(1, i)
+
+        @pl.when(i < CHUNKS - 1)
+        def _():
+            a_load(i + 1, 1).start()
         return carry
 
-    lax.fori_loop(0, CHUNKS, first_up, 0)
+    lax.fori_loop(0, CHUNKS, first_chunk, 0)
     rs2(1, 1)
     rs1(1, 2)
-    rs3(1, 0, g1_out)
+    rs3(0, 1, g2_out)
+    rs2(0, 2)
     rs3(1, 1, g1_out)
     rs2(1, 2)
+    rs3(0, 2, g2_out)
     rs3(1, 2, g1_out)
     slots_v[me] = sq_v[...]
     for copy in exchange_start(me, group_size, slots_v, stat_send, stat_recv):
@@ -533,8 +557,8 @@
 
 
 def moments_kernel(clip_ref, norm_ref, g_one, g_two, g_three, g_four, m_up, m_down, v_up, v_down, m_up_out, m_down_out, v_up_out, v_down_out, u_up, u_down, stats):
-    bias_one = 1.0 - BETA_ONE ** STEP
-    bias_two = 1.0 - BETA_TWO ** STEP
+    inv_one = 1.0 / (1.0 - BETA_ONE ** STEP)
+    inv_two = 1.0 / (1.0 - BETA_TWO ** STEP)
     scale = jnp.minimum(1.0, clip_ref[0] / (jnp.sqrt(norm_ref[0:1, 0:1]) + NORM_EPS))
     row_id = lax.broadcasted_iota(jnp.int32, (8, 128), 0)
     sums = jnp.zeros((8, 128), jnp.float32)
@@ -543,7 +567,7 @@
             grad = grads[layer][...]
             avg_new = BETA_ONE * m[layer] + (1.0 - BETA_ONE) * scale * grad
             sq_new = BETA_TWO * v[layer] + (1.0 - BETA_TWO) * (scale * scale) * (grad * grad)
-            direction = (avg_new / bias_one) / (jnp.sqrt(sq_new / bias_two) + ADAM_EPS)
+            direction = (avg_new * inv_one) / (jnp.sqrt(sq_new * inv_two) + ADAM_EPS)
             m_out[layer] = avg_new
             v_out[layer] = sq_new
             u[layer] = direction
@@ -556,7 +580,7 @@
     stats[...] += sums
 
 
-def moments(clip_norm, norm_tile, grads, m_up, m_down, v_up, v_down, steps=4):
+def moments(clip_norm, norm_tile, grads, m_up, m_down, v_up, v_down, steps=6):
     up, down = m_up.shape, m_down.shape
     up_spec = pl.BlockSpec((2, up[1] // steps, up[2]), lambda i: (0, i, 0))
     down_spec = pl.BlockSpec((2, down[1] // steps, down[2]), lambda i: (0, i, 0))
@@ -684,13 +708,13 @@
     return pl.pallas_call(
         functools.partial(update_kernel, group_size),
         out_shape=[
-            jax.ShapeDtypeStruct((up[0], up[1] * group_size, up[2]), jnp.bfloat16),
-            jax.ShapeDtypeStruct((down[0], down[1] * group_size, down[2]), jnp.bfloat16),
+            pltpu.VMEM((up[0], up[1] * group_size, up[2]), jnp.bfloat16),
+            pltpu.VMEM((down[0], down[1] * group_size, down[2]), jnp.bfloat16),
             jax.ShapeDtypeStruct(up, jnp.float32),
             jax.ShapeDtypeStruct(down, jnp.float32),
         ],
         in_specs=[pl.BlockSpec(memory_space=pltpu.SMEM), vmem] + [hbm] * 4,
-        out_specs=[hbm] * 4,
+        out_specs=[vmem] * 2 + [hbm] * 2,
         scratch_shapes=[
             pltpu.VMEM((group_size, 8, 128), jnp.float32),
             pltpu.VMEM(up, jnp.float32),
@@ -707,7 +731,7 @@
             pltpu.SemaphoreType.DMA((8,)),
             pltpu.SemaphoreType.DMA((4,)),
         ],
-        compiler_params=pltpu.CompilerParams(collective_id=1, has_side_effects=True, vmem_limit_bytes=FULL_VMEM),
+        compiler_params=pltpu.CompilerParams(collective_id=1, has_side_effects=True, vmem_limit_bytes=FULL_VMEM - 2 * group_size * (up[0] * up[1] * up[2] + down[0] * down[1] * down[2]) - 256 * 1024),
         name="update_and_gather",
     )(learn_rate.reshape(1), stats, u_up, u_down, p_up, p_down)
 

time: 430 us -> 419 us (0.974)
  local copies, waits for them, and re-layouts: 21.6 us -> 12.8 us
    unnamed x8, local copies, waits for them, and re-layouts: 20.4 us -> 11.6 us
where the time goes in v4:
time: 419 us
  Pallas kernels  403 us (96%)
  local copies, waits for them, and re-layouts  12.8 us (3%)
    pallas_call x1, Pallas kernels, backward_blocks(): pl.pallas_call(functools.partial(backward_kernel, group_size), out_shape=...  242 us
    pallas_call x1, Pallas kernels, update_and_gather(): pl.pallas_call(functools.partial(update_kernel, group_size), out_shape=[p...  90.2 us
    pallas_call x1, Pallas kernels, forward_block(): pl.pallas_call(forward_kernel, grid=(rows // tile,), out_shape=[jax.Shape...  56.2 us
    pallas_call x1, Pallas kernels, moments(): pl.pallas_call(moments_kernel, grid=(steps,), out_shape=[up_shape, down_s...  14.7 us
    unnamed x8, local copies, waits for them, and re-layouts  11.6 us

profile of v4, /device:TPU:0, one launch (start us, length us, event | category | flops | bytes accessed | tf_op | source)
XLA Modules:
  0.0 419.2 jit_solution(930971378222922901)
XLA Ops:
  0.6 56.2 %forward_block.1 = (bf16[3,4096,1024]{2,1,0:T(8,128)(2,1)}, f32[3,4096,1024]{2,1,0:T(8,128)}, bf16[4096,768]{1,0:T(8,128)(2,1)}) custom-call(bf16[4096,768]{1,0:T(8,128)(2,1)} %x_hbm.1, bf16[2,768,3072]{2,1,0:T(8,128)(2,1)} %w_up_hbm.1, bf16[2,3072,768]{2,1,0:T(8,128)(2,1)} %w_down_hbm.1), custom_call_target="tpu_custom_call" | custom-call | tf_op jit(solution)/shard_map/forward_block/pallas_call | solution.py:98
  56.8 241.5 %backward_blocks.1 = (f32[96,3072]{1,0:T(8,128)}, f32[384,768]{1,0:T(8,128)}, f32[96,3072]{1,0:T(8,128)}, f32[384,768]{1,0:T(8,128)}, f32[8,128]{1,0:T(8,128)}, /*index=5*/bf16[3,4096,1024]{2,1,0:T(8,128)(2,1)}) custom-call(bf16[4096,768]{1,0:T(8,128)(2,1)} %x_hbm.1, bf16[4096,768]{1,0:T(8,128)(2,1)} %e_hbm.1, bf16[4096,768]{1,0:T(8,128)(2,1)} %get-tuple-element.28.h_hbm, ...), custom_call_target="tpu_custom_call" | custom-call | tf_op jit(solution)/shard_map/backward_blocks/pallas_call | solution.py:525
  299.0 14.7 %moments.1 = (f32[2,96,3072]{2,1,0:T(8,128)}, f32[2,384,768]{2,1,0:T(8,128)}, f32[2,96,3072]{2,1,0:T(8,128)}, f32[2,384,768]{2,1,0:T(8,128)}, f32[2,96,3072]{2,1...) custom-call(f32[1]{0:T(128)} %bitcast.4.clip_ref, f32[8,128]{1,0:T(8,128)} %get-tuple-element.31.norm_ref, ...), custom_call_target="tpu_custom_call" | custom-call | tf_op jit(solution)/shard_map/moments/pallas_call | solution.py:592
  314.3 90.2 %update_and_gather.1 = (bf16[2,768,3072]{2,1,0:T(8,128)(2,1)S(1)}, bf16[2,3072,768]{2,1,0:T(8,128)(2,1)S(1)}, f32[2,96,3072]{2,1,0:T(8,128)}, f32[2,384,768]{2,1,0:T(8,128)}) custom-call(f32[1]{0:T(128)} %bitcast.3.rate_ref, f32[8,128]{1,0:T(8,128)} %get-tuple-element.36.stats_ref, f32[2,96,3072]{2,1,0:T(8,128)} %get-tuple-element.37.u_up_hbm, ...), custom_call_target="tpu_custom_call" | custom-call | tf_op jit(solution)/shard_map/update_and_gather/pallas_call | solution.py:708
  404.5 3.7 copy.25
  408.2 0.0 copy-start.1
  408.2 4.0 copy.26
  412.2 1.2 slice.3
  414.1 0.0 copy-done.1
  414.1 0.0 copy-start
  414.1 1.4 copy.29
  415.5 1.1 copy-done
  416.6 1.4 copy.30
Async XLA Ops:
  408.2 5.9 %copy-start.1 = (f32[2,96,3072]{2,1,0:T(8,128)S(1)}, f32[2,96,3072]{2,1,0:T(8,128)}, u32[]{:S(2)}) copy-start(f32[2,96,3072]{2,1,0:T(8,128)} %get-tuple-element.67) | copy-start | bytes 7077892
  414.1 2.5 copy-start

commit v5 on v4

--- a/solution.py
+++ b/solution.py
@@ -162,17 +162,16 @@
 
     def hop0(kind, i):
         if kind == 0:
-            return hop(t_d.at[1 - core], d0.at[i], 0, i, 0, partner)
-        return hop(t_u.at[:, :, 1 - core], u0.at[i], 1, i, 0, partner)
+            return hop(t_d.at[:, 1 - core], d0.at[i], 0, i, 0, partner)
+        return hop(t_u.at[:, :, :, 1 - core], u0.at[i], 1, i, 0, partner)
 
     def bufs(kind):
         return (d0, d1a, d1b, d2a, d2b) if kind == 0 else (u0, u1a, u1b, u2a, u2b)
 
     def hop1(kind, i):
         b0, b1a, b1b, _, _ = bufs(kind)
-        cut = b1a.shape[3]
-        return (hop(b0.at[i, :, 1 - col, :, pl.ds(0, cut)], b1a.at[i], kind, i, 1, near_x),
-                hop(b0.at[i, 1 - row, :, :, pl.ds(cut, cut)], b1b.at[i], kind, i, 2, near_y))
+        return (hop(b0.at[i, 0, :, 1 - col], b1a.at[i], kind, i, 1, near_x),
+                hop(b0.at[i, 1, 1 - row], b1b.at[i], kind, i, 2, near_y))
 
     def hop2(kind, i):
         _, b1a, b1b, b2a, b2b = bufs(kind)
@@ -185,25 +184,25 @@
     def rs1(kind, i):
         hop0(kind, i).wait()
         b0 = bufs(kind)[0]
-        for y in range(2):
-            for x in range(2):
-                own = t_d[core, y, x] if kind == 0 else t_u[y, x, core]
-                b0[i, y, x] = b0[i, y, x] + own
+        for side in range(2):
+            for y in range(2):
+                for x in range(2):
+                    own = t_d[side, core, y, x] if kind == 0 else t_u[side, y, x, core]
+                    b0[i, side, y, x] = b0[i, side, y, x] + own
         for copy in hop1(kind, i):
             copy.start()
 
     def rs2(kind, i):
         b0, b1a, b1b, _, _ = bufs(kind)
-        cut = b1a.shape[3]
         first, second = hop1(kind, i)
         out_a, out_b = hop2(kind, i)
         first.wait()
         for y in range(2):
-            b1a[i, y] = b1a[i, y] + b0[i, y, col, :, 0:cut]
+            b1a[i, y] = b1a[i, y] + b0[i, 0, y, col]
         out_a.start()
         second.wait()
         for x in range(2):
-            b1b[i, x] = b1b[i, x] + b0[i, row, x, :, cut:2 * cut]
+            b1b[i, x] = b1b[i, x] + b0[i, 1, row, x]
         out_b.start()
 
     def rs3(kind, i, out):
@@ -233,16 +232,20 @@
     def grad_down(lhs_ref, rhs_ref, half):
         def part(m, carry):
             acc = dot_tn(lhs_ref[:, at_rows(m * (wide // 2), wide // 2)], rhs_ref[at_rows(half * half_rows, half_rows), :])
-            acc = acc.reshape(t_d.shape[1:])
-            t_d[m] = acc + jnp.where(half == 0, 0.0, t_d[m])
+            cut = dim // 2
+            for side in range(2):
+                piece = acc[:, side * cut:(side + 1) * cut].reshape(t_d.shape[2:])
+                t_d[side, m] = piece + jnp.where(half == 0, 0.0, t_d[side, m])
             return carry
         lax.fori_loop(0, 2, part, 0)
 
     def grad_up(lhs_ref, rhs_ref, half):
         def part(m, carry):
             acc = dot_tn(lhs_ref[at_rows(half * half_rows, half_rows), at_rows(m * (dim // 2), dim // 2)], rhs_ref[...])
-            acc = acc.reshape(t_u.shape[1:])
-            t_u[m] = acc + jnp.where(half == 0, 0.0, t_u[m])
+            cut = wide // 2
+            for side in range(2):
+                piece = acc[:, side * cut:(side + 1) * cut].reshape(t_u.shape[2:])
+                t_u[side, m] = piece + jnp.where(half == 0, 0.0, t_u[side, m])
             return carry
         lax.fori_loop(0, 2, part, 0)
 
@@ -515,7 +518,7 @@
 
     def stages(height, cols):
         return [
-            pltpu.VMEM((CHUNKS, 2, 2, height, cols), f32),
+            pltpu.VMEM((CHUNKS, 2, 2, 2, height, cols // 2), f32),
             pltpu.VMEM((CHUNKS, 2, height, cols // 2), f32),
             pltpu.VMEM((CHUNKS, 2, height, cols // 2), f32),
             pltpu.VMEM((CHUNKS, height, cols // 2), f32),
@@ -535,8 +538,8 @@
             pltpu.VMEM((rows // 2, wide), bf16),
             pltpu.VMEM((rows // 2, wide), bf16),
             pltpu.VMEM((SLOTS, TILE, wide), f32),
-            pltpu.VMEM((2, 2, 2, down_rows, dim), f32),
-            pltpu.VMEM((2, 2, 2, up_rows, wide), f32),
+            pltpu.VMEM((2, 2, 2, 2, down_rows, dim // 2), f32),
+            pltpu.VMEM((2, 2, 2, 2, up_rows, wide // 2), f32),
             *stages(down_rows, dim),
             *stages(up_rows, wide),
             pltpu.VMEM((8, 128), f32),
@@ -580,7 +583,7 @@
     stats[...] += sums
 
 
-def moments(clip_norm, norm_tile, grads, m_up, m_down, v_up, v_down, steps=6):
+def moments(clip_norm, norm_tile, grads, m_up, m_down, v_up, v_down, steps=4):
     up, down = m_up.shape, m_down.shape
     up_spec = pl.BlockSpec((2, up[1] // steps, up[2]), lambda i: (0, i, 0))
     down_spec = pl.BlockSpec((2, down[1] // steps, down[2]), lambda i: (0, i, 0))
@@ -612,6 +615,7 @@
             copy = pltpu.make_async_copy(src.at[layer], dst.at[layer], in_sem.at[len(loads)])
             copy.start()
             loads.append(copy)
+    meet_all(me, group_size)
     row_id = lax.broadcasted_iota(jnp.int32, (8, 128), 0)
     stats = stats_ref[...]
     for index in range(4):
@@ -619,7 +623,6 @@
         master = (p_up, p_down)[index // 2][index % 2]
         stats = stats + jnp.where(row_id == index, jnp.sum(master * master), 0.0)
     slots[me] = stats
-    meet_all(me, group_size)
     for copy in exchange_start(me, group_size, slots, stat_send, stat_recv):
         copy.wait()
     total = slots[0]

time: 419 us -> 417 us (level)
  no operation moved by 1% of the time
where the time goes in v5:
time: 417 us
  Pallas kernels  400 us (96%)
  local copies, waits for them, and re-layouts  12.8 us (3%)
    pallas_call x1, Pallas kernels, backward_blocks(): pl.pallas_call(functools.partial(backward_kernel, group_size), out_shape=...  242 us
    pallas_call x1, Pallas kernels, update_and_gather(): pl.pallas_call(functools.partial(update_kernel, group_size), out_shape=[p...  88.9 us
    pallas_call x1, Pallas kernels, forward_block(): pl.pallas_call(forward_kernel, grid=(rows // tile,), out_shape=[jax.Shape...  56.2 us
    pallas_call x1, Pallas kernels, moments(): pl.pallas_call(moments_kernel, grid=(steps,), out_shape=[up_shape, down_s...  13.8 us
    unnamed x8, local copies, waits for them, and re-layouts  11.6 us

profile of v5, /device:TPU:0, one launch (start us, length us, event | category | flops | bytes accessed | tf_op | source)
XLA Modules:
  0.0 417.1 jit_solution(9775433919503677078)
XLA Ops:
  0.6 56.2 %forward_block.1 = (bf16[3,4096,1024]{2,1,0:T(8,128)(2,1)}, f32[3,4096,1024]{2,1,0:T(8,128)}, bf16[4096,768]{1,0:T(8,128)(2,1)}) custom-call(bf16[4096,768]{1,0:T(8,128)(2,1)} %x_hbm.1, bf16[2,768,3072]{2,1,0:T(8,128)(2,1)} %w_up_hbm.1, bf16[2,3072,768]{2,1,0:T(8,128)(2,1)} %w_down_hbm.1), custom_call_target="tpu_custom_call" | custom-call | tf_op jit(solution)/shard_map/forward_block/pallas_call | solution.py:98
  56.8 241.6 %backward_blocks.1 = (f32[96,3072]{1,0:T(8,128)}, f32[384,768]{1,0:T(8,128)}, f32[96,3072]{1,0:T(8,128)}, f32[384,768]{1,0:T(8,128)}, f32[8,128]{1,0:T(8,128)}, /*index=5*/bf16[3,4096,1024]{2,1,0:T(8,128)(2,1)}) custom-call(bf16[4096,768]{1,0:T(8,128)(2,1)} %x_hbm.1, bf16[4096,768]{1,0:T(8,128)(2,1)} %e_hbm.1, bf16[4096,768]{1,0:T(8,128)(2,1)} %get-tuple-element.28.h_hbm, ...), custom_call_target="tpu_custom_call" | custom-call | tf_op jit(solution)/shard_map/backward_blocks/pallas_call | solution.py:528
  299.1 13.8 %moments.1 = (f32[2,96,3072]{2,1,0:T(8,128)}, f32[2,384,768]{2,1,0:T(8,128)}, f32[2,96,3072]{2,1,0:T(8,128)}, f32[2,384,768]{2,1,0:T(8,128)}, f32[2,96,3072]{2,1...) custom-call(f32[1]{0:T(128)} %bitcast.4.clip_ref, f32[8,128]{1,0:T(8,128)} %get-tuple-element.31.norm_ref, ...), custom_call_target="tpu_custom_call" | custom-call | tf_op jit(solution)/shard_map/moments/pallas_call | solution.py:595
  313.5 88.9 %update_and_gather.1 = (bf16[2,768,3072]{2,1,0:T(8,128)(2,1)S(1)}, bf16[2,3072,768]{2,1,0:T(8,128)(2,1)S(1)}, f32[2,96,3072]{2,1,0:T(8,128)}, f32[2,384,768]{2,1,0:T(8,128)}) custom-call(f32[1]{0:T(128)} %bitcast.3.rate_ref, f32[8,128]{1,0:T(8,128)} %get-tuple-element.36.stats_ref, f32[2,96,3072]{2,1,0:T(8,128)} %get-tuple-element.37.u_up_hbm, ...), custom_call_target="tpu_custom_call" | custom-call | tf_op jit(solution)/shard_map/update_and_gather/pallas_call | solution.py:711
  402.4 3.7 copy.25
  406.1 0.0 copy-start.1
  406.1 4.0 copy.26
  410.1 1.2 slice.3
  412.0 0.0 copy-done.1
  412.0 0.0 copy-start
  412.0 1.4 copy.29
  413.4 1.1 copy-done
  414.5 1.4 copy.30
Async XLA Ops:
  406.1 5.9 %copy-start.1 = (f32[2,96,3072]{2,1,0:T(8,128)S(1)}, f32[2,96,3072]{2,1,0:T(8,128)}, u32[]{:S(2)}) copy-start(f32[2,96,3072]{2,1,0:T(8,128)} %get-tuple-element.67) | copy-start | bytes 7077892
  412.0 2.5 copy-start

commit v6 on v5

--- a/solution.py
+++ b/solution.py
@@ -74,7 +74,12 @@
     return [owner * width + chunk * LANES for owner in OWNERS]
 
 
-def forward_kernel(x_ref, w_up_ref, w_down_ref, a_out, s_out, h_out):
+def forward_kernel(x_ref, w_up_ref, w_down_ref, up_block, down_block_one, down_block_two, a_out, s_out, h_out, down_t_one, down_t_two, up_t):
+    for block, out in ((down_block_one, down_t_one), (down_block_two, down_t_two)):
+        for chunk in range(CHUNKS):
+            out[chunk] = block[0, chunk * LANES:(chunk + 1) * LANES, :].T
+    for chunk in range(CHUNKS):
+        up_t[chunk, 0] = up_block[0, :, chunk * LANES:(chunk + 1) * LANES].T
     x = x_ref[...]
     width = w_up_ref.shape[2] // len(OWNERS)
     total = None
@@ -95,6 +100,13 @@
     rows, dim = act_in.shape
     ff = w_up.shape[2]
     wide = ff // CHUNKS
+    owners = len(OWNERS)
+    width = ff // owners
+    assert rows // tile == owners
+
+    def slot(i):
+        return (i % 2) * (owners // 2) + i // 2
+
     return pl.pallas_call(
         forward_kernel,
         grid=(rows // tile,),
@@ -102,23 +114,32 @@
             jax.ShapeDtypeStruct((CHUNKS, rows, wide), jnp.bfloat16),
             jax.ShapeDtypeStruct((CHUNKS, rows, wide), jnp.float32),
             jax.ShapeDtypeStruct((rows, dim), jnp.bfloat16),
+            jax.ShapeDtypeStruct((CHUNKS, dim, wide), jnp.bfloat16),
+            jax.ShapeDtypeStruct((CHUNKS, dim, wide), jnp.bfloat16),
+            jax.ShapeDtypeStruct((CHUNKS, owners, LANES, dim), jnp.bfloat16),
         ],
         in_specs=[
             pl.BlockSpec((tile, dim), lambda i: (i, 0)),
             pl.BlockSpec((1, dim, ff), lambda i: (0, 0, 0)),
             pl.BlockSpec((1, ff, dim), lambda i: (0, 0, 0)),
+            pl.BlockSpec((1, dim, width), lambda i: (1, 0, i)),
+            pl.BlockSpec((1, width, dim), lambda i: (0, i, 0)),
+            pl.BlockSpec((1, width, dim), lambda i: (1, i, 0)),
         ],
         out_specs=[
             pl.BlockSpec((CHUNKS, tile, wide), lambda i: (0, i, 0)),
             pl.BlockSpec((CHUNKS, tile, wide), lambda i: (0, i, 0)),
             pl.BlockSpec((tile, dim), lambda i: (i, 0)),
+            pl.BlockSpec((CHUNKS, dim, LANES), lambda i: (0, 0, slot(i))),
+            pl.BlockSpec((CHUNKS, dim, LANES), lambda i: (0, 0, slot(i))),
+            pl.BlockSpec((CHUNKS, 1, LANES, dim), lambda i: (0, slot(i), 0, 0)),
         ],
         compiler_params=pltpu.CompilerParams(dimension_semantics=("arbitrary",), vmem_limit_bytes=FULL_VMEM),
         name="forward_block",
-    )(act_in, w_up, w_down)
-
-
-def backward_kernel(group_size, x_hbm, e_hbm, h_hbm, a_hbm, s_hbm, w_up_hbm, w_down_hbm,
+    )(act_in, w_up, w_down, w_up, w_down, w_down)
+
+
+def backward_kernel(group_size, x_hbm, e_hbm, h_hbm, a_hbm, s_hbm, w_up_hbm, down_t_one, down_t_two, up_t,
                     g1_out, g2_out, g3_out, g4_out, norm_out, q_hbm,
                     h_v, e_v, wu_v, wd_v, a_v, q_v, s_v, t_d, t_u,
                     d0, d1a, d1b, d2a, d2b, u0, u1a, u1b, u2a, u2b,
@@ -139,21 +160,25 @@
         span = pl.ds(half * half_rows, half_rows)
         return pltpu.make_async_copy(src.at[span], dst.at[span], load_sem.at[sem, half])
 
-    def start_weight(which, chunk, layer):
+    def start_up(chunk):
         for j, start in enumerate(chunk_blocks(chunk, width)):
-            if which == 0:
-                pltpu.make_async_copy(w_up_hbm.at[layer, :, pl.ds(start, LANES)], wu_v.at[chunk, :, pl.ds(j * LANES, LANES)], w_sem.at[0, chunk]).start()
-            else:
-                pltpu.make_async_copy(w_down_hbm.at[layer, pl.ds(start, LANES), :], wd_v.at[chunk, pl.ds(j * LANES, LANES), :], w_sem.at[1, chunk]).start()
+            pltpu.make_async_copy(w_up_hbm.at[1, :, pl.ds(start, LANES)], wu_v.at[chunk, :, pl.ds(j * LANES, LANES)], w_sem.at[0, chunk]).start()
+
+    def start_down(src, chunk):
+        pltpu.make_async_copy(src.at[chunk], wd_v.at[chunk], w_sem.at[1, chunk]).start()
+
+    def up_t_copy(part):
+        span = (pl.ds(0, half_rows), pl.ds(half_rows, CHUNKS * wide - half_rows))[part]
+        return pltpu.make_async_copy(up_t.at[span], e_v.at[span], load_sem.at[1, part])
 
     def wait_weight(which, chunk):
         ref = (wu_v, wd_v)[which]
         pltpu.make_async_copy(ref.at[chunk], ref.at[chunk], w_sem.at[which, chunk]).wait()
 
     half_copy(h_hbm, h_v, 0, 0).start()
-    start_weight(0, 0, 1)
+    start_up(0)
     half_copy(e_hbm, e_v, 0, 1).start()
-    start_weight(1, 0, 1)
+    start_down(down_t_two, 0)
     sq_v[...] = jnp.zeros_like(sq_v)
     meet_all(me, group_size)
 
@@ -263,8 +288,8 @@
             half_copy(h_hbm, h_v, 1, 0).start()
             half_copy(e_hbm, e_v, 1, 1).start()
             for chunk in range(1, CHUNKS):
-                start_weight(0, chunk, 1)
-                start_weight(1, chunk, 1)
+                start_up(chunk)
+                start_down(down_t_two, chunk)
 
         def second_half(half, carry):
             @pl.when((i == 0) & (half == 1))
@@ -279,48 +304,56 @@
             def second_tile(t, carry):
                 span = at_rows(half * half_rows + t * TILE, TILE)
                 z = dot_nn(h_v[span, :], wu_v[i])
-                p = dot_nt(e_v[span, :], wd_v[i])
+                p = dot_nn(e_v[span, :], wd_v[i])
                 gelu, slope = gelu_parts(z)
                 here = at_rows(t * TILE, TILE)
                 a_v[here, :] = gelu.astype(jnp.bfloat16)
                 q_v[here, :] = (p * slope).astype(jnp.bfloat16)
 
-                @pl.when((half == 0) & (i > 1))
-                def _():
-                    @pl.when(t == 0)
-                    def _():
-                        rs2(1, i - 2)
-
-                    @pl.when(t == 2)
-                    def _():
-                        rs3(0, i - 2, g4_out)
-
-                @pl.when((t == tiles // 2) & (half == 0) & (i > 0))
+                @pl.when((t == 0) & (half == 0) & (i > 1))
+                def _():
+                    rs3(1, i - 2, g3_out)
+                    give_free(i - 2)
+
+                @pl.when((t == 1) & (half == 0) & (i > 0))
                 def _():
                     rs1(0, i - 1)
 
-                @pl.when((t == 3) & (half == 1) & (i > 0))
+                @pl.when((t == 5) & (half == 0) & (i > 0))
+                def _():
+                    rs1(1, i - 1)
+
+                @pl.when((t == 0) & (half == 1) & (i > 0))
                 def _():
                     rs2(0, i - 1)
+
+                @pl.when((t == 6) & (half == 1) & (i > 0))
+                def _():
+                    rs2(1, i - 1)
                 return carry
 
             lax.fori_loop(0, tiles, second_tile, 0)
             q_copy(i, half).start()
 
-            @pl.when((half == 0) & (i > 1))
-            def _():
-                rs3(1, i - 2, g3_out)
-                give_free(i - 2)
-
             grad_down(a_v, e_v, half)
 
+            @pl.when(i == CHUNKS - 1)
+            def _():
+                @pl.when(half == 0)
+                def _():
+                    up_t_copy(0).start()
+
+                @pl.when(half == 1)
+                def _():
+                    up_t_copy(1).start()
+
             @pl.when(half == 1)
             def _():
                 rs0(0, i)
 
-            @pl.when((half == 0) & (i > 0))
-            def _():
-                rs1(1, i - 1)
+                @pl.when(i > 0)
+                def _():
+                    rs3(0, i - 1, g4_out)
 
             grad_up(h_v, q_v, half)
 
@@ -335,10 +368,8 @@
     lax.fori_loop(0, CHUNKS, second_chunk, 0)
 
     q_copy(CHUNKS - 1, 1).wait()
-    for half in range(2):
-        half_copy(x_hbm, e_v, half, 1).start()
     for chunk in range(CHUNKS):
-        start_weight(1, chunk, 0)
+        start_down(down_t_one, chunk)
     r_rows = half_rows // 4
     staging = (a_v, q_v)
 
@@ -359,9 +390,9 @@
             pltpu.make_async_copy(whole, whole, load_sem.at[2, slot]).wait()
             for part in range(2):
                 m = part * (r_rows // 2)
-                acc = dot_nt(staging[slot][m:m + r_rows // 2, :], wu_v[0])
+                acc = dot_nn(staging[slot][m:m + r_rows // 2, :], e_v[0:wide, :])
                 for k in range(1, CHUNKS):
-                    acc = acc + dot_nt(staging[slot][k * r_rows + m:k * r_rows + m + r_rows // 2, :], wu_v[k])
+                    acc = acc + dot_nn(staging[slot][k * r_rows + m:k * r_rows + m + r_rows // 2, :], e_v[k * wide:(k + 1) * wide, :])
                 h_v[at_rows((2 * t + slot) * r_rows + m, r_rows // 2), :] = acc.astype(jnp.bfloat16)
 
             @pl.when(t < r_steps - 1)
@@ -371,17 +402,20 @@
         @pl.when(t == 0)
         def _():
             rs1(0, CHUNKS - 1)
-            rs3(0, CHUNKS - 2, g4_out)
-
-        @pl.when(t == 1)
-        def _():
             rs1(1, CHUNKS - 1)
-            rs3(1, CHUNKS - 2, g3_out)
-            give_free(CHUNKS - 2)
+
+        @pl.when(t == 2)
+        def _():
+            rs2(0, CHUNKS - 1)
         return carry
 
-    rs2(1, CHUNKS - 2)
+    rs3(1, CHUNKS - 2, g3_out)
+    give_free(CHUNKS - 2)
+    for part in range(2):
+        up_t_copy(part).wait()
     lax.fori_loop(0, r_steps, r_pair, 0)
+    for half in range(2):
+        half_copy(x_hbm, e_v, half, 1).start()
     for half in range(2):
         a_load(0, half).start()
 
@@ -391,9 +425,12 @@
 
     for t in range(slots):
         s_load(0, t).start()
-    rs2(0, CHUNKS - 1)
 
     def first_chunk(i, carry):
+        @pl.when(i == 1)
+        def _():
+            rs2(0, 0)
+
         a_load(i, 0).wait()
         grad_down(a_v, h_v, 0)
 
@@ -401,9 +438,13 @@
         def _():
             a_load(i + 1, 0).start()
 
+        @pl.when(i == 0)
+        def _():
+            rs2(1, 2)
+
         @pl.when(i == 2)
         def _():
-            rs2(1, 0)
+            rs2(0, 1)
 
         a_load(i, 1).wait()
         grad_down(q_v, h_v, 1)
@@ -420,7 +461,7 @@
             def first_tile(t, carry):
                 tt = half * tiles + t
                 s_load(i, tt).wait()
-                p = dot_nt(h_v[at_rows(tt * TILE, TILE), :], wd_v[i])
+                p = dot_nn(h_v[at_rows(tt * TILE, TILE), :], wd_v[i])
                 q_v[at_rows(t * TILE, TILE), :] = (p * s_v[lax.rem(tt, slots)]).astype(jnp.bfloat16)
 
                 ahead = tt + slots
@@ -428,45 +469,33 @@
                 def _():
                     s_load(i, ahead).start()
 
-                @pl.when((tt == 6) & (i == 0))
-                def _():
-                    rs3(0, 2, g4_out)
-
-                @pl.when((tt == tiles + 3) & (i == 2))
-                def _():
-                    rs3(1, 0, g1_out)
-                return carry
-
-            @pl.when(half == 0)
-            def _():
-                @pl.when(i == 0)
-                def _():
-                    rs2(1, 2)
-
-                @pl.when(i == 1)
-                def _():
-                    rs2(0, 0)
-
-                @pl.when(i > 0)
-                def _():
-                    rs1(1, i - 1)
-
-            @pl.when(half == 1)
-            def _():
-                @pl.when(i == 2)
-                def _():
-                    rs2(0, 1)
-
-                rs1(0, i)
-
-                @pl.when(i == 0)
+                @pl.when((tt == 7) & (i == 0))
                 def _():
                     rs3(1, 2, g3_out)
                     give_free(2)
 
+                @pl.when((tt == tiles + 6) & (i == 1))
+                def _():
+                    rs2(1, 0)
+                return carry
+
+            @pl.when(half == 0)
+            def _():
+                @pl.when(i > 0)
+                def _():
+                    rs1(1, i - 1)
+
+                @pl.when(i == 0)
+                def _():
+                    rs3(0, 2, g4_out)
+
                 @pl.when(i == 1)
                 def _():
                     rs3(0, 0, g2_out)
+
+                @pl.when(i == 2)
+                def _():
+                    rs3(1, 0, g1_out)
 
             lax.fori_loop(0, tiles, first_tile, 0)
 
@@ -474,6 +503,14 @@
             def _():
                 for t in range(slots):
                     s_load(i + 1, t).start()
+
+            @pl.when(half == 0)
+            def _():
+                rs1(0, i)
+
+                @pl.when(i == 2)
+                def _():
+                    rs3(0, 1, g2_out)
 
             grad_up(e_v, q_v, half)
             return carry
@@ -489,7 +526,6 @@
     lax.fori_loop(0, CHUNKS, first_chunk, 0)
     rs2(1, 1)
     rs1(1, 2)
-    rs3(0, 1, g2_out)
     rs2(0, 2)
     rs3(1, 1, g1_out)
     rs2(1, 2)
@@ -504,7 +540,7 @@
     norm_out[...] = jnp.full(norm_out.shape, jnp.sum(total))
 
 
-def backward_blocks(group_size, act_in, grad_out, hidden, act_one, slope_one, w_up, w_down):
+def backward_blocks(group_size, act_in, grad_out, hidden, act_one, slope_one, w_up, down_t_one, down_t_two, up_t):
     rows, dim = act_in.shape
     ff = w_up.shape[2]
     wide = ff // CHUNKS
@@ -528,13 +564,13 @@
     return pl.pallas_call(
         functools.partial(backward_kernel, group_size),
         out_shape=[up_grad, down_grad, up_grad, down_grad, jax.ShapeDtypeStruct((8, 128), f32), jax.ShapeDtypeStruct((CHUNKS, rows, wide), bf16)],
-        in_specs=[hbm] * 7,
+        in_specs=[hbm] * 9,
         out_specs=[vmem] * 5 + [hbm],
         scratch_shapes=[
             pltpu.VMEM((rows, dim), bf16),
             pltpu.VMEM((rows, dim), bf16),
             pltpu.VMEM((CHUNKS, dim, wide), bf16),
-            pltpu.VMEM((CHUNKS, wide, dim), bf16),
+            pltpu.VMEM((CHUNKS, dim, wide), bf16),
             pltpu.VMEM((rows // 2, wide), bf16),
             pltpu.VMEM((rows // 2, wide), bf16),
             pltpu.VMEM((SLOTS, TILE, wide), f32),
@@ -556,7 +592,7 @@
         ],
         compiler_params=pltpu.CompilerParams(collective_id=2, has_side_effects=True, vmem_limit_bytes=FULL_VMEM),
         name="backward_blocks",
-    )(act_in, grad_out, hidden, act_one, slope_one, w_up, w_down)[:5]
+    )(act_in, grad_out, hidden, act_one, slope_one, w_up, down_t_one, down_t_two, up_t.reshape(ff, dim))[:5]
 
 
 def moments_kernel(clip_ref, norm_ref, g_one, g_two, g_three, g_four, m_up, m_down, v_up, v_down, m_up_out, m_down_out, v_up_out, v_down_out, u_up, u_down, stats):
@@ -746,8 +782,8 @@
     replicated = P()
 
     def device_step(act_in, grad_out, w_up, w_down, master_up, master_down, exp_avg_up, exp_avg_down, exp_sq_up, exp_sq_down, learn_rate, clip_norm):
-        act_one, slope_one, hidden = forward_block(act_in, w_up, w_down)
-        *grads, norm_tile = backward_blocks(group_size, act_in, grad_out, hidden, act_one, slope_one, w_up, w_down)
+        act_one, slope_one, hidden, *turned = forward_block(act_in, w_up, w_down)
+        *grads, norm_tile = backward_blocks(group_size, act_in, grad_out, hidden, act_one, slope_one, w_up, *turned)
         grad_norm = jnp.sqrt(norm_tile[0, 0])
         avg_up, avg_down, sq_up, sq_down, dir_up, dir_down, stats = moments(clip_norm, norm_tile, grads, exp_avg_up, exp_avg_down, exp_sq_up, exp_sq_down)
         new_w_up, new_w_down, master_up_out, master_down_out = update_and_gather(group_size, learn_rate, stats, dir_up, dir_down, master_up, master_down)

time: 417 us -> 413 us (level)
    pallas_call x1, Pallas kernels: 242 us -> 235 us  [backward_blocks(): pl.pallas_call(functools.partial(backward_kernel, group_size), out_shape=...]
where the time goes in v6:
time: 413 us; the launch traced here: 412 us
  Pallas kernels  396 us (96%)
  local copies, waits for them, and re-layouts  12.8 us (3%)
    pallas_call x1, Pallas kernels, backward_blocks(): pl.pallas_call(functools.partial(backward_kernel, group_size), out_shape=...  235 us
    pallas_call x1, Pallas kernels, update_and_gather(): pl.pallas_call(functools.partial(update_kernel, group_size), out_shape=[p...  88.8 us
    pallas_call x1, Pallas kernels, forward_block(): pl.pallas_call(forward_kernel, grid=(rows // tile,), out_shape=[jax.Shape...  58 us
    pallas_call x1, Pallas kernels, moments(): pl.pallas_call(moments_kernel, grid=(steps,), out_shape=[up_shape, down_s...  13.8 us
    unnamed x8, local copies, waits for them, and re-layouts  11.6 us

profile of v6, /device:TPU:0, one launch (start us, length us, event | category | flops | bytes accessed | tf_op | source)
XLA Modules:
  0.0 412.5 jit_solution(5578574778703828255)
XLA Ops:
  0.6 58.0 %forward_block.1 = (bf16[3,4096,1024]{2,1,0:T(8,128)(2,1)}, f32[3,4096,1024]{2,1,0:T(8,128)}, bf16[4096,768]{1,0:T(8,128)(2,1)}, bf16[3,768,1024]{2,1,0:T(8,128)...) custom-call(bf16[4096,768]{1,0:T(8,128)(2,1)} %x_hbm.1, bf16[2,768,3072]{2,1,0:T(8,128)(2,1)} %w_up_hbm.1, ...), custom_call_target="tpu_custom_call" | custom-call | tf_op jit(solution)/shard_map/forward_block/pallas_call | solution.py:110
  58.7 235.2 %backward_blocks.1 = (f32[96,3072]{1,0:T(8,128)}, f32[384,768]{1,0:T(8,128)}, f32[96,3072]{1,0:T(8,128)}, f32[384,768]{1,0:T(8,128)}, f32[8,128]{1,0:T(8,128)}, /*index=5*/bf16[3,4096,1024]{2,1,0:T(8,128)(2,1)}) custom-call(bf16[4096,768]{1,0:T(8,128)(2,1)} %x_hbm.1, bf16[4096,768]{1,0:T(8,128)(2,1)} %e_hbm.1, bf16[4096,768]{1,0:T(8,128)(2,1)} %get-tuple-element.31.h_hbm, ...), custom_call_target="tpu_custom_call" | custom-call | tf_op jit(solution)/shard_map/backward_blocks/pallas_call | solution.py:564
  294.6 13.8 %moments.1 = (f32[2,96,3072]{2,1,0:T(8,128)}, f32[2,384,768]{2,1,0:T(8,128)}, f32[2,96,3072]{2,1,0:T(8,128)}, f32[2,384,768]{2,1,0:T(8,128)}, f32[2,96,3072]{2,1...) custom-call(f32[1]{0:T(128)} %bitcast.5.clip_ref, f32[8,128]{1,0:T(8,128)} %get-tuple-element.37.norm_ref, ...), custom_call_target="tpu_custom_call" | custom-call | tf_op jit(solution)/shard_map/moments/pallas_call | solution.py:631
  309.0 88.8 %update_and_gather.1 = (bf16[2,768,3072]{2,1,0:T(8,128)(2,1)S(1)}, bf16[2,3072,768]{2,1,0:T(8,128)(2,1)S(1)}, f32[2,96,3072]{2,1,0:T(8,128)}, f32[2,384,768]{2,1,0:T(8,128)}) custom-call(f32[1]{0:T(128)} %bitcast.4.rate_ref, f32[8,128]{1,0:T(8,128)} %get-tuple-element.42.stats_ref, f32[2,96,3072]{2,1,0:T(8,128)} %get-tuple-element.43.u_up_hbm, ...), custom_call_target="tpu_custom_call" | custom-call | tf_op jit(solution)/shard_map/update_and_gather/pallas_call | solution.py:747
  397.8 3.7 copy.25
  401.5 0.0 copy-start.1
  401.5 4.0 copy.26
  405.5 1.2 slice.3
  407.4 0.0 copy-done.1
  407.4 0.0 copy-start
  407.4 1.4 copy.29
  408.8 1.1 copy-done
  409.9 1.4 copy.30
Async XLA Ops:
  401.5 5.9 %copy-start.1 = (f32[2,96,3072]{2,1,0:T(8,128)S(1)}, f32[2,96,3072]{2,1,0:T(8,128)}, u32[]{:S(2)}) copy-start(f32[2,96,3072]{2,1,0:T(8,128)} %get-tuple-element.73) | copy-start | bytes 7077892
  407.4 2.5 copy-start

commit v7 on v6

--- a/solution.py
+++ b/solution.py
@@ -51,19 +51,19 @@
 
 
 CHUNKS = 3
+HALVES = range(2)
+DOWN, UP = HALVES
+FIRST, SECOND, THIRD = range(CHUNKS)
+ZERO = 0.0
 LANES = 128
 TILE = 256
 SLOTS = 4
-OWNERS = tuple(chip * 2 + core for core in range(2) for chip in range(4))
+OWNERS = tuple(chip * 2 + core for core in HALVES for chip in range(4))
 FULL_VMEM = 67043328
 
 
 def dot_nn(lhs, rhs):
     return jnp.dot(lhs, rhs, preferred_element_type=jnp.float32)
-
-
-def dot_nt(lhs, rhs):
-    return lax.dot_general(lhs, rhs, (((1,), (1,)), ((), ())), preferred_element_type=jnp.float32)
 
 
 def dot_tn(lhs, rhs):
@@ -140,10 +140,10 @@
 
 
 def backward_kernel(group_size, x_hbm, e_hbm, h_hbm, a_hbm, s_hbm, w_up_hbm, down_t_one, down_t_two, up_t,
-                    g1_out, g2_out, g3_out, g4_out, norm_out, q_hbm,
-                    h_v, e_v, wu_v, wd_v, a_v, q_v, s_v, t_d, t_u,
+                    g1_hbm, g2_hbm, g3_hbm, g4_hbm, norm_out, q_hbm,
+                    g1_out, g2_out, g3_out, g4_out, h_v, e_v, wu_v, wd_v, a_v, q_v, s_v, t_d, t_u,
                     d0, d1a, d1b, d2a, d2b, u0, u1a, u1b, u2a, u2b,
-                    sq_v, slots_v, load_sem, w_sem, q_sem, s_sem, send_sem, recv_sem, free_sem, stat_send, stat_recv):
+                    sq_v, slots_v, load_sem, w_sem, q_sem, s_sem, send_sem, recv_sem, free_sem, stat_send, stat_recv, out_sem):
     me, partner, near_x, near_y = coords()
     core, col, row = me % 2, (me // 2) % 2, me // 4
     rows, dim = h_v.shape
@@ -186,12 +186,12 @@
         return remote(src, dst, send_sem.at[kind, chunk, stage], recv_sem.at[kind, chunk, stage], device)
 
     def hop0(kind, i):
-        if kind == 0:
+        if kind == DOWN:
             return hop(t_d.at[:, 1 - core], d0.at[i], 0, i, 0, partner)
         return hop(t_u.at[:, :, :, 1 - core], u0.at[i], 1, i, 0, partner)
 
     def bufs(kind):
-        return (d0, d1a, d1b, d2a, d2b) if kind == 0 else (u0, u1a, u1b, u2a, u2b)
+        return (d0, d1a, d1b, d2a, d2b) if kind == DOWN else (u0, u1a, u1b, u2a, u2b)
 
     def hop1(kind, i):
         b0, b1a, b1b, _, _ = bufs(kind)
@@ -209,10 +209,10 @@
     def rs1(kind, i):
         hop0(kind, i).wait()
         b0 = bufs(kind)[0]
-        for side in range(2):
-            for y in range(2):
-                for x in range(2):
-                    own = t_d[side, core, y, x] if kind == 0 else t_u[side, y, x, core]
+        for side in HALVES:
+            for y in HALVES:
+                for x in HALVES:
+                    own = t_d[side, core, y, x] if kind == DOWN else t_u[side, y, x, core]
                     b0[i, side, y, x] = b0[i, side, y, x] + own
         for copy in hop1(kind, i):
             copy.start()
@@ -222,11 +222,11 @@
         first, second = hop1(kind, i)
         out_a, out_b = hop2(kind, i)
         first.wait()
-        for y in range(2):
+        for y in HALVES:
             b1a[i, y] = b1a[i, y] + b0[i, 0, y, col]
         out_a.start()
         second.wait()
-        for x in range(2):
+        for x in HALVES:
             b1b[i, x] = b1b[i, x] + b0[i, 1, row, x]
         out_b.start()
 
@@ -240,7 +240,7 @@
         square = (left * left + right * right).reshape(left.shape[0] // 8, 8, cut).sum(axis=0)
         for lane in range(0, cut, LANES):
             sq_v[...] += square[:, lane:lane + LANES]
-        if kind == 0:
+        if kind == DOWN:
             span = at_rows(i * LANES, LANES)
             out[span, 0:cut] = left
             out[span, cut:2 * cut] = right
@@ -250,6 +250,9 @@
                 lane = (j % 4) * LANES
                 out[:, pl.ds(pl.multiple_of(owner * width + i * LANES, LANES), LANES)] = part[:, lane:lane + LANES]
 
+    results = tuple(pltpu.make_async_copy(src, dst, out_sem.at[k]) for k, (src, dst) in enumerate(((g1_out, g1_hbm), (g2_out, g2_hbm), (g3_out, g3_hbm), (g4_out, g4_hbm))))
+    g1_copy, g2_copy, g3_copy, g4_copy = results
+
     def give_free(i):
         for device in (partner, near_x, near_y):
             pl.semaphore_signal(free_sem.at[i], inc=1, device_id=(device,), device_id_type=MESH)
@@ -258,9 +261,9 @@
         def part(m, carry):
             acc = dot_tn(lhs_ref[:, at_rows(m * (wide // 2), wide // 2)], rhs_ref[at_rows(half * half_rows, half_rows), :])
             cut = dim // 2
-            for side in range(2):
+            for side in HALVES:
                 piece = acc[:, side * cut:(side + 1) * cut].reshape(t_d.shape[2:])
-                t_d[side, m] = piece + jnp.where(half == 0, 0.0, t_d[side, m])
+                t_d[side, m] = piece + jnp.where(half == FIRST, ZERO, t_d[side, m])
             return carry
         lax.fori_loop(0, 2, part, 0)
 
@@ -268,9 +271,9 @@
         def part(m, carry):
             acc = dot_tn(lhs_ref[at_rows(half * half_rows, half_rows), at_rows(m * (dim // 2), dim // 2)], rhs_ref[...])
             cut = wide // 2
-            for side in range(2):
+            for side in HALVES:
                 piece = acc[:, side * cut:(side + 1) * cut].reshape(t_u.shape[2:])
-                t_u[side, m] = piece + jnp.where(half == 0, 0.0, t_u[side, m])
+                t_u[side, m] = piece + jnp.where(half == FIRST, ZERO, t_u[side, m])
             return carry
         lax.fori_loop(0, 2, part, 0)
 
@@ -281,7 +284,7 @@
         wait_weight(0, i)
         wait_weight(1, i)
 
-        @pl.when(i == 0)
+        @pl.when(i == FIRST)
         def _():
             half_copy(h_hbm, h_v, 0, 0).wait()
             half_copy(e_hbm, e_v, 0, 1).wait()
@@ -292,12 +295,12 @@
                 start_down(down_t_two, chunk)
 
         def second_half(half, carry):
-            @pl.when((i == 0) & (half == 1))
+            @pl.when((i == FIRST) & (half == SECOND))
             def _():
                 half_copy(h_hbm, h_v, 1, 0).wait()
                 half_copy(e_hbm, e_v, 1, 1).wait()
 
-            @pl.when((i > 0) | (half > 0))
+            @pl.when((i > FIRST) | (half > 0))
             def _():
                 q_copy(i, half).wait()
 
@@ -310,26 +313,26 @@
                 a_v[here, :] = gelu.astype(jnp.bfloat16)
                 q_v[here, :] = (p * slope).astype(jnp.bfloat16)
 
-                @pl.when((t == 0) & (half == 0) & (i > 1))
-                def _():
-                    rs3(1, i - 2, g3_out)
+                @pl.when((t == 0) & (half == FIRST) & (i > SECOND))
+                def _():
+                    rs3(UP, i - 2, g3_out)
                     give_free(i - 2)
 
-                @pl.when((t == 1) & (half == 0) & (i > 0))
-                def _():
-                    rs1(0, i - 1)
-
-                @pl.when((t == 5) & (half == 0) & (i > 0))
-                def _():
-                    rs1(1, i - 1)
-
-                @pl.when((t == 0) & (half == 1) & (i > 0))
-                def _():
-                    rs2(0, i - 1)
-
-                @pl.when((t == 6) & (half == 1) & (i > 0))
-                def _():
-                    rs2(1, i - 1)
+                @pl.when((t == 1) & (half == FIRST) & (i > FIRST))
+                def _():
+                    rs1(DOWN, i - 1)
+
+                @pl.when((t == 5) & (half == FIRST) & (i > FIRST))
+                def _():
+                    rs1(UP, i - 1)
+
+                @pl.when((t == 0) & (half == SECOND) & (i > FIRST))
+                def _():
+                    rs2(DOWN, i - 1)
+
+                @pl.when((t == 6) & (half == SECOND) & (i > FIRST))
+                def _():
+                    rs2(UP, i - 1)
                 return carry
 
             lax.fori_loop(0, tiles, second_tile, 0)
@@ -337,29 +340,29 @@
 
             grad_down(a_v, e_v, half)
 
-            @pl.when(i == CHUNKS - 1)
+            @pl.when(i == THIRD)
             def _():
-                @pl.when(half == 0)
+                @pl.when(half == FIRST)
                 def _():
                     up_t_copy(0).start()
 
-                @pl.when(half == 1)
+                @pl.when(half == SECOND)
                 def _():
                     up_t_copy(1).start()
 
-            @pl.when(half == 1)
+            @pl.when(half == SECOND)
             def _():
-                rs0(0, i)
-
-                @pl.when(i > 0)
-                def _():
-                    rs3(0, i - 1, g4_out)
+                rs0(DOWN, i)
+
+                @pl.when(i > FIRST)
+                def _():
+                    rs3(DOWN, i - 1, g4_out)
 
             grad_up(h_v, q_v, half)
 
-            @pl.when(half == 1)
+            @pl.when(half == SECOND)
             def _():
-                rs0(1, i)
+                rs0(UP, i)
             return carry
 
         lax.fori_loop(0, 2, second_half, 0)
@@ -367,7 +370,7 @@
 
     lax.fori_loop(0, CHUNKS, second_chunk, 0)
 
-    q_copy(CHUNKS - 1, 1).wait()
+    q_copy(THIRD, 1).wait()
     for chunk in range(CHUNKS):
         start_down(down_t_one, chunk)
     r_rows = half_rows // 4
@@ -380,15 +383,15 @@
     def a_load(i, half):
         return pltpu.make_async_copy(a_hbm.at[i, pl.ds(half * half_rows, half_rows), :], staging[half], load_sem.at[0, half])
 
-    for slot in range(2):
+    for slot in HALVES:
         r_load(slot, slot)
     r_steps = rows // r_rows // 2
 
     def r_pair(t, carry):
-        for slot in range(2):
+        for slot in HALVES:
             whole = staging[slot].at[pl.ds(0, CHUNKS * r_rows), :]
             pltpu.make_async_copy(whole, whole, load_sem.at[2, slot]).wait()
-            for part in range(2):
+            for part in HALVES:
                 m = part * (r_rows // 2)
                 acc = dot_nn(staging[slot][m:m + r_rows // 2, :], e_v[0:wide, :])
                 for k in range(1, CHUNKS):
@@ -401,22 +404,22 @@
 
         @pl.when(t == 0)
         def _():
-            rs1(0, CHUNKS - 1)
-            rs1(1, CHUNKS - 1)
+            rs1(DOWN, THIRD)
+            rs1(UP, THIRD)
 
         @pl.when(t == 2)
         def _():
-            rs2(0, CHUNKS - 1)
+            rs2(DOWN, THIRD)
         return carry
 
-    rs3(1, CHUNKS - 2, g3_out)
-    give_free(CHUNKS - 2)
-    for part in range(2):
+    rs3(UP, SECOND, g3_out)
+    give_free(SECOND)
+    for part in HALVES:
         up_t_copy(part).wait()
     lax.fori_loop(0, r_steps, r_pair, 0)
-    for half in range(2):
+    for half in HALVES:
         half_copy(x_hbm, e_v, half, 1).start()
-    for half in range(2):
+    for half in HALVES:
         a_load(0, half).start()
 
     def s_load(i, t):
@@ -427,34 +430,34 @@
         s_load(0, t).start()
 
     def first_chunk(i, carry):
-        @pl.when(i == 1)
+        @pl.when(i == SECOND)
         def _():
-            rs2(0, 0)
+            rs2(DOWN, FIRST)
 
         a_load(i, 0).wait()
         grad_down(a_v, h_v, 0)
 
-        @pl.when(i < CHUNKS - 1)
+        @pl.when(i < THIRD)
         def _():
             a_load(i + 1, 0).start()
 
-        @pl.when(i == 0)
+        @pl.when(i == FIRST)
         def _():
-            rs2(1, 2)
-
-        @pl.when(i == 2)
+            rs2(UP, THIRD)
+
+        @pl.when(i == THIRD)
         def _():
-            rs2(0, 1)
+            rs2(DOWN, SECOND)
 
         a_load(i, 1).wait()
         grad_down(q_v, h_v, 1)
         pl.semaphore_wait(free_sem.at[i], 3)
-        rs0(0, i)
+        rs0(DOWN, i)
         wait_weight(1, i)
 
-        @pl.when(i == 0)
+        @pl.when(i == FIRST)
         def _():
-            for half in range(2):
+            for half in HALVES:
                 half_copy(x_hbm, e_v, half, 1).wait()
 
         def first_half(half, carry):
@@ -469,68 +472,72 @@
                 def _():
                     s_load(i, ahead).start()
 
-                @pl.when((tt == 7) & (i == 0))
-                def _():
-                    rs3(1, 2, g3_out)
-                    give_free(2)
-
-                @pl.when((tt == tiles + 6) & (i == 1))
-                def _():
-                    rs2(1, 0)
+                @pl.when((tt == 7) & (i == FIRST))
+                def _():
+                    rs3(UP, THIRD, g3_out)
+                    give_free(THIRD)
+                    g3_copy.start()
+                    g4_copy.start()
+
+                @pl.when((tt == tiles + 6) & (i == SECOND))
+                def _():
+                    rs2(UP, FIRST)
                 return carry
 
-            @pl.when(half == 0)
+            @pl.when(half == FIRST)
             def _():
-                @pl.when(i > 0)
-                def _():
-                    rs1(1, i - 1)
-
-                @pl.when(i == 0)
-                def _():
-                    rs3(0, 2, g4_out)
-
-                @pl.when(i == 1)
-                def _():
-                    rs3(0, 0, g2_out)
-
-                @pl.when(i == 2)
-                def _():
-                    rs3(1, 0, g1_out)
+                @pl.when(i > FIRST)
+                def _():
+                    rs1(UP, i - 1)
+
+                @pl.when(i == FIRST)
+                def _():
+                    rs3(DOWN, THIRD, g4_out)
+
+                @pl.when(i == SECOND)
+                def _():
+                    rs3(DOWN, FIRST, g2_out)
+
+                @pl.when(i == THIRD)
+                def _():
+                    rs3(UP, FIRST, g1_out)
 
             lax.fori_loop(0, tiles, first_tile, 0)
 
-            @pl.when((half == 1) & (i < CHUNKS - 1))
+            @pl.when((half == SECOND) & (i < THIRD))
             def _():
                 for t in range(slots):
                     s_load(i + 1, t).start()
 
-            @pl.when(half == 0)
+            @pl.when(half == FIRST)
             def _():
-                rs1(0, i)
-
-                @pl.when(i == 2)
-                def _():
-                    rs3(0, 1, g2_out)
+                rs1(DOWN, i)
+
+                @pl.when(i == THIRD)
+                def _():
+                    rs3(DOWN, SECOND, g2_out)
 
             grad_up(e_v, q_v, half)
             return carry
 
         lax.fori_loop(0, 2, first_half, 0)
-        rs0(1, i)
-
-        @pl.when(i < CHUNKS - 1)
+        rs0(UP, i)
+
+        @pl.when(i < THIRD)
         def _():
             a_load(i + 1, 1).start()
         return carry
 
     lax.fori_loop(0, CHUNKS, first_chunk, 0)
-    rs2(1, 1)
-    rs1(1, 2)
-    rs2(0, 2)
-    rs3(1, 1, g1_out)
-    rs2(1, 2)
-    rs3(0, 2, g2_out)
-    rs3(1, 2, g1_out)
+    rs2(UP, SECOND)
+    rs1(UP, THIRD)
+    rs2(DOWN, THIRD)
+    rs3(UP, SECOND, g1_out)
+    rs2(UP, THIRD)
+    rs3(DOWN, THIRD, g2_out)
+    g2_copy.start()
+    rs3(UP, THIRD, g1_out)
+    g1_copy.start()
     slots_v[me] = sq_v[...]
     for copy in exchange_start(me, group_size, slots_v, stat_send, stat_recv):
         copy.wait()
@@ -538,6 +545,8 @@
     for index in range(1, group_size):
         total = total + slots_v[index]
     norm_out[...] = jnp.full(norm_out.shape, jnp.sum(total))
+    for copy in results:
+        copy.wait()
 
 
 def backward_blocks(group_size, act_in, grad_out, hidden, act_one, slope_one, w_up, down_t_one, down_t_two, up_t):
@@ -565,8 +574,9 @@
         functools.partial(backward_kernel, group_size),
         out_shape=[up_grad, down_grad, up_grad, down_grad, jax.ShapeDtypeStruct((8, 128), f32), jax.ShapeDtypeStruct((CHUNKS, rows, wide), bf16)],
         in_specs=[hbm] * 9,
-        out_specs=[vmem] * 5 + [hbm],
+        out_specs=[hbm] * 4 + [vmem, hbm],
         scratch_shapes=[
+            *(pltpu.VMEM(g.shape, f32) for g in (up_grad, down_grad, up_grad, down_grad)),
             pltpu.VMEM((rows, dim), bf16),
             pltpu.VMEM((rows, dim), bf16),
             pltpu.VMEM((CHUNKS, dim, wide), bf16),
@@ -589,20 +599,22 @@
             pltpu.SemaphoreType.REGULAR((CHUNKS,)),
             pltpu.SemaphoreType.DMA((group_size,)),
             pltpu.SemaphoreType.DMA((group_size,)),
+            pltpu.SemaphoreType.DMA((4,)),
         ],
         compiler_params=pltpu.CompilerParams(collective_id=2, has_side_effects=True, vmem_limit_bytes=FULL_VMEM),
         name="backward_blocks",
     )(act_in, grad_out, hidden, act_one, slope_one, w_up, down_t_one, down_t_two, up_t.reshape(ff, dim))[:5]
 
 
-def moments_kernel(clip_ref, norm_ref, g_one, g_two, g_three, g_four, m_up, m_down, v_up, v_down, m_up_out, m_down_out, v_up_out, v_down_out, u_up, u_down, stats):
+def moments_kernel(clip_ref, norm_ref, g_one, g_two, g_three, g_four, m_up, m_down, v_up, v_down, m_up_out, m_down_out, v_up_out, v_down_out, u_up, u_down, stats, norm_out):
     inv_one = 1.0 / (1.0 - BETA_ONE ** STEP)
     inv_two = 1.0 / (1.0 - BETA_TWO ** STEP)
+    norm_out[0] = jnp.sqrt(norm_ref[0, 0])
     scale = jnp.minimum(1.0, clip_ref[0] / (jnp.sqrt(norm_ref[0:1, 0:1]) + NORM_EPS))
     row_id = lax.broadcasted_iota(jnp.int32, (8, 128), 0)
     sums = jnp.zeros((8, 128), jnp.float32)
     for family, (grads, m, v, m_out, v_out, u) in enumerate([((g_one, g_three), m_up, v_up, m_up_out, v_up_out, u_up), ((g_two, g_four), m_down, v_down, m_down_out, v_down_out, u_down)]):
-        for layer in range(2):
+        for layer in HALVES:
             grad = grads[layer][...]
             avg_new = BETA_ONE * m[layer] + (1.0 - BETA_ONE) * scale * grad
             sq_new = BETA_TWO * v[layer] + (1.0 - BETA_TWO) * (scale * scale) * (grad * grad)
@@ -631,9 +643,9 @@
     return pl.pallas_call(
         moments_kernel,
         grid=(steps,),
-        out_shape=[up_shape, down_shape] * 3 + [jax.ShapeDtypeStruct((8, 128), jnp.float32)],
+        out_shape=[up_shape, down_shape] * 3 + [jax.ShapeDtypeStruct((8, 128), jnp.float32), jax.ShapeDtypeStruct((1,), jnp.float32)],
         in_specs=[pl.BlockSpec(memory_space=pltpu.SMEM), tile] + [up_grad, down_grad] * 2 + pair * 2,
-        out_specs=pair * 3 + [tile],
+        out_specs=pair * 3 + [tile, pl.BlockSpec(memory_space=pltpu.SMEM)],
         compiler_params=pltpu.CompilerParams(dimension_semantics=("arbitrary",), vmem_limit_bytes=FULL_VMEM),
         name="moments",
     )(clip_norm.reshape(1), norm_tile, *grads, m_up, m_down, v_up, v_down)
@@ -647,7 +659,7 @@
     me, partner, near_x, near_y = coords()
     loads = []
     for src, dst in ((p_up_hbm, p_up), (p_down_hbm, p_down), (u_up_hbm, u_up), (u_down_hbm, u_down)):
-        for layer in range(2):
+        for layer in HALVES:
             copy = pltpu.make_async_copy(src.at[layer], dst.at[layer], in_sem.at[len(loads)])
             copy.start()
             loads.append(copy)
@@ -715,19 +727,19 @@
     for piece in (0, 1):
         forward(own[piece], piece, me, near_y, 4)
     diag = near_x + near_y - me
-    for k in range(2):
+    for k in HALVES:
         spot = arrival(k, 2, near_x)
         forward(spot, k, near_x, near_y, 6)
         forward(spot, k, near_x, partner, 3)
         spot = arrival(2 + k, 4, near_y)
         forward(spot, 2 + k, near_y, near_x, 6)
         forward(spot, 2 + k, near_y, partner, 5)
-    for k in range(2):
+    for k in HALVES:
         spot = arrival(2 + k, 2, near_x)
         forward(spot, 2 + k, near_x, partner, 3)
         spot = arrival(k, 4, near_y)
         forward(spot, k, near_y, partner, 5)
-    for k in range(2):
+    for k in HALVES:
         for piece in (2 + k, k):
             spot = arrival(piece, 6, diag)
             forward(spot, piece, diag, partner, 7)
@@ -784,9 +796,8 @@
     def device_step(act_in, grad_out, w_up, w_down, master_up, master_down, exp_avg_up, exp_avg_down, exp_sq_up, exp_sq_down, learn_rate, clip_norm):
         act_one, slope_one, hidden, *turned = forward_block(act_in, w_up, w_down)
         *grads, norm_tile = backward_blocks(group_size, act_in, grad_out, hidden, act_one, slope_one, w_up, *turned)
-        grad_norm = jnp.sqrt(norm_tile[0, 0])
-        avg_up, avg_down, sq_up, sq_down, dir_up, dir_down, stats = moments(clip_norm, norm_tile, grads, exp_avg_up, exp_avg_down, exp_sq_up, exp_sq_down)
+        avg_up, avg_down, sq_up, sq_down, dir_up, dir_down, stats, norm_value = moments(clip_norm, norm_tile, grads, exp_avg_up, exp_avg_down, exp_sq_up, exp_sq_down)
         new_w_up, new_w_down, master_up_out, master_down_out = update_and_gather(group_size, learn_rate, stats, dir_up, dir_down, master_up, master_down)
-        return (new_w_up, new_w_down, master_up_out, master_down_out, avg_up, avg_down, sq_up, sq_down, grad_norm)
+        return (new_w_up, new_w_down, master_up_out, master_down_out, avg_up, avg_down, sq_up, sq_down, norm_value.reshape(()))
 
     return jax.shard_map(device_step, mesh=mesh, in_specs=(batch_rows, batch_rows, replicated, replicated, state_rows, state_rows, state_rows, state_rows, state_rows, state_rows, replicated, replicated), out_specs=(replicated, replicated, state_rows, state_rows, state_rows, state_rows, state_rows, state_rows, replicated), check_vma=False)

time: 413 us -> 408 us (0.988)
  no operation moved by 1% of the time
where the time goes in v7:
time: 408 us
  Pallas kernels  395 us (97%)
  local copies, waits for them, and re-layouts  11.6 us (3%)
    pallas_call x1, Pallas kernels, backward_blocks(): pl.pallas_call(functools.partial(backward_kernel, group_size), out_shape=...  234 us
    pallas_call x1, Pallas kernels, update_and_gather(): pl.pallas_call(functools.partial(update_kernel, group_size), out_shape=[p...  88.8 us
    pallas_call x1, Pallas kernels, forward_block(): pl.pallas_call(forward_kernel, grid=(rows // tile,), out_shape=[jax.Shape...  58 us
    pallas_call x1, Pallas kernels, moments(): pl.pallas_call(moments_kernel, grid=(steps,), out_shape=[up_shape, down_s...  13.8 us
    unnamed x8, local copies, waits for them, and re-layouts  11.6 us

profile of v7, /device:TPU:0, one launch (start us, length us, event | category | flops | bytes accessed | tf_op | source)
XLA Modules:
  0.0 408.1 jit_solution(1226969327875817770)
XLA Ops:
  0.6 58.0 %forward_block.1 = (bf16[3,4096,1024]{2,1,0:T(8,128)(2,1)}, f32[3,4096,1024]{2,1,0:T(8,128)}, bf16[4096,768]{1,0:T(8,128)(2,1)}, bf16[3,768,1024]{2,1,0:T(8,128)...) custom-call(bf16[4096,768]{1,0:T(8,128)(2,1)} %x_hbm.1, bf16[2,768,3072]{2,1,0:T(8,128)(2,1)} %w_up_hbm.1, ...), custom_call_target="tpu_custom_call" | custom-call | tf_op jit(solution)/shard_map/forward_block/pallas_call | solution.py:110
  58.7 233.9 %backward_blocks.1 = (f32[96,3072]{1,0:T(8,128)}, f32[384,768]{1,0:T(8,128)}, f32[96,3072]{1,0:T(8,128)}, f32[384,768]{1,0:T(8,128)}, f32[8,128]{1,0:T(8,128)}, /*index=5*/bf16[3,4096,1024]{2,1,0:T(8,128)(2,1)}) custom-call(bf16[4096,768]{1,0:T(8,128)(2,1)} %x_hbm.1, bf16[4096,768]{1,0:T(8,128)(2,1)} %e_hbm.1, bf16[4096,768]{1,0:T(8,128)(2,1)} %get-tuple-element.32.h_hbm, ...), custom_call_target="tpu_custom_call" | custom-call | tf_op jit(solution)/shard_map/backward_blocks/pallas_call | solution.py:573
  293.2 13.8 %moments.1 = (f32[2,96,3072]{2,1,0:T(8,128)}, f32[2,384,768]{2,1,0:T(8,128)}, f32[2,96,3072]{2,1,0:T(8,128)}, f32[2,384,768]{2,1,0:T(8,128)}, f32[2,96,3072]{2,1...) custom-call(f32[1]{0:T(128)} %bitcast.5.clip_ref, f32[8,128]{1,0:T(8,128)} %get-tuple-element.38.norm_ref, ...), custom_call_target="tpu_custom_call" | custom-call | tf_op jit(solution)/shard_map/moments/pallas_call | solution.py:643
  307.7 88.8 %update_and_gather.1 = (bf16[2,768,3072]{2,1,0:T(8,128)(2,1)S(1)}, bf16[2,3072,768]{2,1,0:T(8,128)(2,1)S(1)}, f32[2,96,3072]{2,1,0:T(8,128)}, f32[2,384,768]{2,1,0:T(8,128)}) custom-call(f32[1]{0:T(128)} %bitcast.4.rate_ref, f32[8,128]{1,0:T(8,128)} %get-tuple-element.43.stats_ref, f32[2,96,3072]{2,1,0:T(8,128)} %get-tuple-element.44.u_up_hbm, ...), custom_call_target="tpu_custom_call" | custom-call | tf_op jit(solution)/shard_map/update_and_gather/pallas_call | solution.py:759
  396.5 3.7 copy.25
  400.2 0.0 copy-start.1
  400.2 4.0 copy.26
  404.2 0.0 copy-done.1
  404.2 0.0 copy-start
  404.2 1.4 copy.29
  405.6 1.1 copy-done
  406.7 1.4 copy.30
Async XLA Ops:
  400.2 4.0 copy-start.1
  404.2 2.5 copy-start

commit v8 on v7

--- a/solution.py
+++ b/solution.py
@@ -479,9 +479,9 @@
                     g3_copy.start()
                     g4_copy.start()
 
-                @pl.when((tt == tiles + 6) & (i == SECOND))
-                def _():
-                    rs2(UP, FIRST)
+                @pl.when((tt == tiles + 6) & (i > FIRST))
+                def _():
+                    rs2(UP, i - 1)
                 return carry
 
             @pl.when(half == FIRST)
@@ -529,9 +529,8 @@
         return carry
 
     lax.fori_loop(0, CHUNKS, first_chunk, 0)
-    rs2(UP, SECOND)
+    rs2(DOWN, THIRD)
     rs1(UP, THIRD)
-    rs2(DOWN, THIRD)
     rs3(UP, SECOND, g1_out)
     rs2(UP, THIRD)
     rs3(DOWN, THIRD, g2_out)

time: 408 us -> 409 us (level)
  no operation moved by 1% of the time
where the time goes in v8:
time: 409 us
  Pallas kernels  396 us (97%)
  local copies, waits for them, and re-layouts  11.6 us (3%)
    pallas_call x1, Pallas kernels, backward_blocks(): pl.pallas_call(functools.partial(backward_kernel, group_size), out_shape=...  236 us
    pallas_call x1, Pallas kernels, update_and_gather(): pl.pallas_call(functools.partial(update_kernel, group_size), out_shape=[p...  88 us
    pallas_call x1, Pallas kernels, forward_block(): pl.pallas_call(forward_kernel, grid=(rows // tile,), out_shape=[jax.Shape...  58 us
    pallas_call x1, Pallas kernels, moments(): pl.pallas_call(moments_kernel, grid=(steps,), out_shape=[up_shape, down_s...  13.8 us
    unnamed x8, local copies, waits for them, and re-layouts  11.6 us

profile of v8, /device:TPU:0, one launch (start us, length us, event | category | flops | bytes accessed | tf_op | source)
XLA Modules:
  0.0 409.1 jit_solution(13074101803601304559)
XLA Ops:
  0.6 58.0 %forward_block.1 = (bf16[3,4096,1024]{2,1,0:T(8,128)(2,1)}, f32[3,4096,1024]{2,1,0:T(8,128)}, bf16[4096,768]{1,0:T(8,128)(2,1)}, bf16[3,768,1024]{2,1,0:T(8,128)...) custom-call(bf16[4096,768]{1,0:T(8,128)(2,1)} %x_hbm.1, bf16[2,768,3072]{2,1,0:T(8,128)(2,1)} %w_up_hbm.1, ...), custom_call_target="tpu_custom_call" | custom-call | tf_op jit(solution)/shard_map/forward_block/pallas_call | solution.py:110
  58.7 235.7 %backward_blocks.1 = (f32[96,3072]{1,0:T(8,128)}, f32[384,768]{1,0:T(8,128)}, f32[96,3072]{1,0:T(8,128)}, f32[384,768]{1,0:T(8,128)}, f32[8,128]{1,0:T(8,128)}, /*index=5*/bf16[3,4096,1024]{2,1,0:T(8,128)(2,1)}) custom-call(bf16[4096,768]{1,0:T(8,128)(2,1)} %x_hbm.1, bf16[4096,768]{1,0:T(8,128)(2,1)} %e_hbm.1, bf16[4096,768]{1,0:T(8,128)(2,1)} %get-tuple-element.32.h_hbm, ...), custom_call_target="tpu_custom_call" | custom-call | tf_op jit(solution)/shard_map/backward_blocks/pallas_call | solution.py:572
  295.0 13.8 %moments.1 = (f32[2,96,3072]{2,1,0:T(8,128)}, f32[2,384,768]{2,1,0:T(8,128)}, f32[2,96,3072]{2,1,0:T(8,128)}, f32[2,384,768]{2,1,0:T(8,128)}, f32[2,96,3072]{2,1...) custom-call(f32[1]{0:T(128)} %bitcast.5.clip_ref, f32[8,128]{1,0:T(8,128)} %get-tuple-element.38.norm_ref, ...), custom_call_target="tpu_custom_call" | custom-call | tf_op jit(solution)/shard_map/moments/pallas_call | solution.py:642
  309.5 88.0 %update_and_gather.1 = (bf16[2,768,3072]{2,1,0:T(8,128)(2,1)S(1)}, bf16[2,3072,768]{2,1,0:T(8,128)(2,1)S(1)}, f32[2,96,3072]{2,1,0:T(8,128)}, f32[2,384,768]{2,1,0:T(8,128)}) custom-call(f32[1]{0:T(128)} %bitcast.4.rate_ref, f32[8,128]{1,0:T(8,128)} %get-tuple-element.43.stats_ref, f32[2,96,3072]{2,1,0:T(8,128)} %get-tuple-element.44.u_up_hbm, ...), custom_call_target="tpu_custom_call" | custom-call | tf_op jit(solution)/shard_map/update_and_gather/pallas_call | solution.py:758
  397.5 3.7 copy.25
  401.2 0.0 copy-start.1
  401.2 4.0 copy.26
  405.2 0.0 copy-done.1
  405.2 0.0 copy-start
  405.2 1.4 copy.29
  406.6 1.1 copy-done
  407.7 1.4 copy.30
Async XLA Ops:
  401.2 4.0 copy-start.1
  405.2 2.5 copy-start
